TPU v7x, 32 devices: a whole 2x2x4 slice. The times are simulated.
32 devices in a mesh: tok: 8 (over z, y), rep: 4 (over x, core).
Axes of the slice: x: 2, y: 2, z: 4, core: 2. Of those that a mesh axis runs over, the one named last changes fastest.
Arguments:
- patches: bfloat16 [8192, 768], P(('tok', 'rep')), may hold values from -6 to 6
- patch_view: int32 [8192], P(('tok', 'rep')), may hold values from 0 to 511
- rays: bfloat16 [8192, 768], P(('tok', 'rep')), may hold values from -6 to 6
- ray_view: int32 [8192], P(('tok', 'rep')), may hold values from 0 to 511
- targets: float32 [3, 8192], P(None, ('tok', 'rep')), may hold values from -6 to 6
- camera: bfloat16 [512, 768], P('tok'), may hold values from -6 to 6
- slots_init: float32 [64, 768], replicated, may hold values from -6 to 6
- key_weight: bfloat16 [768, 768], P('tok'), may hold values from -0.875 to 0.875
- value_weight: bfloat16 [768, 768], P('tok'), may hold values from -0.4375 to 0.4375
- query_weight: bfloat16 [768, 768], P('tok'), may hold values from -0.21875 to 0.21875
- gru_input: bfloat16 [768, 2304], P('tok'), may hold values from -0.21875 to 0.21875
- gru_hidden: bfloat16 [768, 2304], P('tok'), may hold values from -0.21875 to 0.21875
- mix_query: bfloat16 [768, 768], P('tok'), may hold values from -0.875 to 0.875
- mix_key: bfloat16 [768, 768], P('tok'), may hold values from -0.21875 to 0.21875
- render_in: bfloat16 [768, 1536], P('tok'), may hold values from -0.21875 to 0.21875
- render_out: bfloat16 [3, 1536], P(None, 'tok'), may hold values from -0.15625 to 0.15625
Outputs:
- slots_out: float32 [64, 768], replicated
- colour: float32 [3, 8192], P(None, ('tok', 'rep'))
- loss: float32 [], replicated
- grad_render_in: float32 [768, 1536], P('tok')
- grad_render_out: float32 [3, 1536], replicated
All inputs are finite; a program needn't handle non-finite values.
Results may differ from a plain program's by a relative error of at most 0.019.
Values may be sent and summed in bfloat16 or wider, within the bound.
No kernel may reach another device: no remote copies, remote signals or barrier semaphores. Data moves between devices by JAX's collectives and lax.ppermute only.
A program may use at most 128 MiB of HBM per device.

v0:
```python
import jax
import jax.numpy as jnp
from jax import lax
from jax.sharding import PartitionSpec as P

ITERS = 3


EPSILON = 1e-05
ATTN_FLOOR = 1e-08


def normalize(values):
    mean = jnp.mean(values, axis=-1, keepdims=True)
    centred = values - mean
    spread = jnp.mean(centred * centred, axis=-1, keepdims=True)
    return centred * lax.rsqrt(spread + EPSILON)


def lookup(table, index):
    onehot = (index[:, None] == jnp.arange(table.shape[0], dtype=jnp.int32)[None, :]).astype(
        jnp.bfloat16
    )
    return jnp.dot(onehot, table, preferred_element_type=jnp.float32)


def slot_update(slots, update, gru_input, gru_hidden):
    width = slots.shape[1]
    from_update = jnp.dot(
        update.astype(jnp.bfloat16), gru_input, preferred_element_type=jnp.float32
    )
    from_state = jnp.dot(slots.astype(jnp.bfloat16), gru_hidden, preferred_element_type=jnp.float32)
    reset = jax.nn.sigmoid(from_update[:, :width] + from_state[:, :width])
    blend = jax.nn.sigmoid(from_update[:, width : 2 * width] + from_state[:, width : 2 * width])
    candidate = jnp.tanh(from_update[:, 2 * width :] + reset * from_state[:, 2 * width :])
    return (1.0 - blend) * candidate + blend * slots


def add_rows(left, piece):
    return jnp.dot(left, piece, preferred_element_type=jnp.float32)


def on_device(
    patches,
    patch_view,
    rays,
    ray_view,
    targets,
    camera,
    slots_init,
    key_weight,
    value_weight,
    query_weight,
    gru_input,
    gru_hidden,
    mix_query,
    mix_key,
    render_in,
    render_out,
):
    width = patches.shape[1]
    scale = width ** (-0.5)
    table = lax.all_gather(camera, "tok", axis=0, tiled=True)
    patch_in = patches.astype(jnp.float32) + lookup(table, patch_view)
    patch_x = normalize(patch_in).astype(jnp.bfloat16)
    keys_sum = add_rows(patch_x, lax.all_gather(key_weight, "tok", axis=0, tiled=True))
    values_sum = add_rows(patch_x, lax.all_gather(value_weight, "tok", axis=0, tiled=True))
    keys = keys_sum.astype(jnp.bfloat16)
    values = values_sum.astype(jnp.bfloat16)
    query_full, input_full, hidden_full, mixkey_full, colour_full = (
        lax.all_gather(query_weight, "tok", axis=0, tiled=True),
        lax.all_gather(gru_input, "tok", axis=0, tiled=True),
        lax.all_gather(gru_hidden, "tok", axis=0, tiled=True),
        lax.all_gather(mix_key, "tok", axis=0, tiled=True),
        lax.all_gather(render_out, "tok", axis=1, tiled=True),
    )
    slots = slots_init
    for step in range(ITERS):
        query = (
            jnp.dot(
                normalize(slots).astype(jnp.bfloat16),
                query_full,
                preferred_element_type=jnp.float32,
            )
            * scale
        ).astype(jnp.bfloat16)
        logits = lax.dot_general(
            keys, query, (((1,), (1,)), ((), ())), preferred_element_type=jnp.float32
        )
        attn = jax.nn.softmax(logits, axis=1) + ATTN_FLOOR
        numer = lax.dot_general(
            attn.astype(jnp.bfloat16),
            values,
            (((0,), (0,)), ((), ())),
            preferred_element_type=jnp.float32,
        )
        denom = jnp.sum(attn, axis=0)
        numer, denom = lax.psum((numer, denom), ("tok", "rep"))
        slots = slot_update(slots, numer / denom[:, None], input_full, hidden_full)
    slots_low = slots.astype(jnp.bfloat16)
    ray_in = rays.astype(jnp.float32) + lookup(table, ray_view)
    ray_x = ray_in.astype(jnp.bfloat16)
    ray_rows = ray_x.shape[0]
    query_sum = add_rows(ray_x, lax.all_gather(mix_query, "tok", axis=0, tiled=True))
    ray_query = (query_sum * scale).astype(jnp.bfloat16)
    slot_keys = jnp.dot(slots_low, mixkey_full, preferred_element_type=jnp.float32).astype(
        jnp.bfloat16
    )
    mix_logits = lax.dot_general(
        ray_query, slot_keys, (((1,), (1,)), ((), ())), preferred_element_type=jnp.float32
    )
    mix = jax.nn.softmax(mix_logits, axis=1).astype(jnp.bfloat16)
    joined = (jnp.dot(mix, slots_low, preferred_element_type=jnp.float32) + ray_in).astype(
        jnp.bfloat16
    )
    pre = add_rows(joined, lax.all_gather(render_in, "tok", axis=0, tiled=True))
    hidden = jax.nn.silu(pre).astype(jnp.bfloat16)
    colour = lax.dot_general(
        colour_full, hidden, (((1,), (1,)), ((), ())), preferred_element_type=jnp.float32
    )
    error = colour - targets
    rays_total = ray_rows * lax.axis_size("tok") * lax.axis_size("rep")
    dcol = (error * (2.0 / jnp.sqrt(jnp.float32(3.0 * rays_total)))).astype(jnp.bfloat16)
    squared = jnp.sum(error * error)
    out_part = jnp.dot(dcol, hidden, preferred_element_type=jnp.float32)
    squared, grad_render_out = lax.psum((squared, out_part), ("tok", "rep"))
    loss = squared / (3.0 * rays_total)
    dhidden = lax.dot_general(
        dcol, colour_full, (((0,), (0,)), ((), ())), preferred_element_type=jnp.float32
    )
    sig = jax.nn.sigmoid(pre)
    dpre = (dhidden * (sig + pre * sig * (1.0 - sig))).astype(jnp.bfloat16)
    mine = lax.psum_scatter(
        lax.dot_general(joined, dpre, (((0,), (0,)), ((), ())), preferred_element_type=jnp.float32),
        ("tok", "rep"),
        scatter_dimension=0,
        tiled=True,
    )
    grad_render_in = lax.all_gather(mine, "rep", axis=0, tiled=True)
    return (slots, colour, loss, grad_render_in, grad_render_out)


def solution(mesh):
    placed = (
        P(("tok", "rep"), None),
        P(("tok", "rep")),
        P(("tok", "rep"), None),
        P(("tok", "rep")),
        P(None, ("tok", "rep")),
        P("tok", None),
        P(),
        P("tok", None),
        P("tok", None),
        P("tok", None),
        P("tok", None),
        P("tok", None),
        P("tok", None),
        P("tok", None),
        P("tok", None),
        P(None, "tok"),
    )
    return jax.shard_map(
        on_device,
        mesh=mesh,
        in_specs=placed,
        out_specs=(P(), P(None, ("tok", "rep")), P(), P("tok", None), P()),
        check_vma=False,
    )
```

profile of v0, /device:TPU:0, one launch (start us, length us, event | category | flops | bytes accessed | tf_op | source)
XLA Modules:
  0.0 937.6 jit_solution(16529850342338148391)
XLA Ops:
  7.2 0.7 all-gather.10.cloned.1.call-update
  8.0 0.7 all-gather.12.cloned.1.call-update
  8.7 0.7 all-gather.14.cloned.1.call-update
  9.4 0.5 all-gather.18.cloned.1.call-update
  10.0 1.0 reduce_sum.146
  11.1 1.1 multiply_reduce_fusion.3
  12.2 35.5 %all_gather.33 = bf16[512,768]{1,0:T(8,128)(2,1)S(1)} all-gather(bf16[64,768]{1,0:T(8,128)(2,1)} %param.21), channel_id=1, replica_groups=mesh['tok'=8,'rep'=4] {'tok'}, dimensions={0}, use_global_device_ids=true | all-gather | bytes 884736 | tf_op jit(solution)/shard_map/all_gather | solution.py:63
  47.7 1.0 copy-done.2
  48.6 0.5 fusion.112
  49.1 0.2 multiply_reduce_fusion
  49.4 7.3 all-gather.10.cloned.1.call-done
  56.7 1.8 convolution_convert_fusion.1
  58.5 40.5 %all-gather.12.cloned.1.call-done = bf16[768,768]{1,0:T(8,128)(2,1)} async-done(((bf16[96,768]{1,0:T(8,128)(2,1)}), bf16[768,768]{1,0:T(8,128)(2,1)}) %all-gather.12.cloned.1.call-update) | async-done | bytes 1179664 | tf_op jit(solution)/shard_map/all_gather | solution.py:71
  99.0 1.8 fusion.113
  100.9 40.1 %all-gather.14.cloned.1.call-done = bf16[768,768]{1,0:T(8,128)(2,1)} async-done(((bf16[96,768]{1,0:T(8,128)(2,1)}), bf16[768,768]{1,0:T(8,128)(2,1)}) %all-gather.14.cloned.1.call-update) | async-done | bytes 1179664 | tf_op jit(solution)/shard_map/all_gather | solution.py:67
  141.0 1.8 convolution_convert_fusion
  142.8 0.9 fusion.95
  143.8 0.5 all-gather.16.cloned.1.call-update
  144.5 40.1 %psum.57 = f32[64]{0:T(128)S(1)} all-reduce(f32[64]{0:T(128)S(1)} %fusion.97), channel_id=1, replica_groups=mesh['tok'=8,'rep'=4] {'tok','rep'}, use_global_device_ids=true, to_apply=%region_8.0 | all-reduce | flops 64 | bytes 512 | tf_op jit(solution)/shard_map/psum | solution.py:98
  184.6 23.1 %all-gather.18.cloned.1.call-done = bf16[768,2304]{1,0:T(8,128)(2,1)} async-done(((bf16[96,2304]{1,0:T(8,128)(2,1)}), bf16[768,2304]{1,0:T(8,128)(2,1)}) %all-gather.18.cloned.1.call-update) | async-done | bytes 3538960 | tf_op jit(solution)/shard_map/all_gather | solution.py:73
  207.7 2.7 fusion.73
  210.4 126.7 %all-reduce.5.cloned.1.call-done = f32[64,768]{1,0:T(8,128)} async-done(((f32[64,768]{1,0:T(8,128)}), f32[64,768]{1,0:T(8,128)}) %all-reduce.5.cloned.1.call-update) | async-done | bytes 196624 | tf_op jit(solution)/shard_map/psum | solution.py:98
  337.2 67.6 %all-gather.16.cloned.1.call-done = bf16[768,2304]{1,0:T(8,128)(2,1)} async-done(((bf16[96,2304]{1,0:T(8,128)(2,1)}), bf16[768,2304]{1,0:T(8,128)(2,1)}) %all-gather.16.cloned.1.call-update) | async-done | bytes 3538960 | tf_op jit(solution)/shard_map/all_gather | solution.py:72
  404.7 2.9 fusion.56
  407.7 0.2 fusion.110
  407.9 0.2 multiply_reduce_fusion.2
  408.1 0.9 copy-done.1
  409.0 0.6 fusion.114
  409.6 0.9 fusion.93
  410.6 3.8 fusion.66
  414.6 39.3 %psum.59 = f32[64]{0:T(128)S(1)} all-reduce(f32[64]{0:T(128)S(1)} %fusion.98), channel_id=1, replica_groups=mesh['tok'=8,'rep'=4] {'tok','rep'}, use_global_device_ids=true, to_apply=%region_15.0 | all-reduce | flops 64 | bytes 512 | tf_op jit(solution)/shard_map/psum | solution.py:98
  453.8 80.3 %all-reduce.7.cloned.1.call-done = f32[64,768]{1,0:T(8,128)} async-done(((f32[64,768]{1,0:T(8,128)}), f32[64,768]{1,0:T(8,128)}) %all-reduce.7.cloned.1.call-update) | async-done | bytes 196624 | tf_op jit(solution)/shard_map/psum | solution.py:98
  534.2 1.8 fusion.57
  536.0 0.2 fusion.108
  536.3 0.7 copy-done.6
  536.9 0.2 multiply_reduce_fusion.1
  537.1 2.7 fusion.115
  539.8 0.9 fusion.85
  540.7 1.9 fusion.91
  542.7 0.7 all-gather.22.cloned.1.call-update
  543.4 0.5 all-gather.20.cloned.1.call-update
  544.0 0.7 all-gather.24.cloned.1.call-update
  544.8 27.1 %all-gather = bf16[8,192,3]{1,2,0:T(4,128)(2,1)S(1)} all-gather(bf16[1,192,3]{1,2,0:T(4,128)(2,1)S(1)} %bitcast.38), channel_id=1, replica_groups=mesh['tok'=8,'rep'=4] {'tok'}, dimensions={0}, use_global_device_ids=true | all-gather | bytes 10368 | tf_op jit(solution)/shard_map/all_gather | solution.py:75
  571.9 0.7 reshape.72
  572.6 2.6 convolution_add_fusion
  575.3 38.2 %psum.61 = f32[64]{0:T(128)S(1)} all-reduce(f32[64]{0:T(128)S(1)} %fusion.99), channel_id=1, replica_groups=mesh['tok'=8,'rep'=4] {'tok','rep'}, use_global_device_ids=true, to_apply=%region_22.0 | all-reduce | flops 64 | bytes 512 | tf_op jit(solution)/shard_map/psum | solution.py:98
  613.5 3.7 fusion.59
  617.2 51.2 %all-reduce.9.cloned.1.call-done = f32[64,768]{1,0:T(8,128)} async-done(((f32[64,768]{1,0:T(8,128)}), f32[64,768]{1,0:T(8,128)}) %all-reduce.9.cloned.1.call-update) | async-done | bytes 196624 | tf_op jit(solution)/shard_map/psum | solution.py:98
  668.4 1.8 fusion.58
  670.2 0.1 fusion.23
  670.4 42.3 %all-gather.22.cloned.1.call-done = bf16[768,768]{1,0:T(8,128)(2,1)} async-done(((bf16[96,768]{1,0:T(8,128)(2,1)}), bf16[768,768]{1,0:T(8,128)(2,1)}) %all-gather.22.cloned.1.call-update) | async-done | bytes 1179664 | tf_op jit(solution)/shard_map/all_gather | solution.py:74
  712.7 1.6 convolution_convert_fusion.2
  714.3 40.3 %all-gather.20.cloned.1.call-done = bf16[768,768]{1,0:T(8,128)(2,1)} async-done(((bf16[96,768]{1,0:T(8,128)(2,1)}), bf16[768,768]{1,0:T(8,128)(2,1)}) %all-gather.20.cloned.1.call-update) | async-done | bytes 1179664 | tf_op jit(solution)/shard_map/all_gather | solution.py:104
  754.6 2.0 fusion.116
  756.6 0.3 fusion.3
  756.9 50.4 %all-gather.24.cloned.1.call-done = bf16[768,1536]{1,0:T(8,128)(2,1)} async-done(((bf16[96,1536]{1,0:T(8,128)(2,1)}), bf16[768,1536]{1,0:T(8,128)(2,1)}) %all-gather.24.cloned.1.call-update) | async-done | bytes 2359312 | tf_op jit(solution)/shard_map/all_gather | solution.py:116
  807.3 2.5 fusion.13
  809.8 1.5 multiply_convert_fusion.10
  811.3 3.5 fusion.1
  814.9 0.2 fusion.119
  815.1 39.8 %all-reduce = (f32[]{:T(128)}, f32[3,1536]{1,0:T(4,128)}) all-reduce(f32[]{:T(128)} %get-tuple-element.12, f32[3,1536]{1,0:T(4,128)S(1)} %fusion.119), channel_id=1, replica_groups=mesh['tok'=8,'rep'=4] {'tok','rep'}, use_global_device_ids=true, to_apply=%region_26.27 | all-reduce | flops 4609 | bytes 36872 | tf_op jit(solution)/shard_map/psum | solution.py:126
  855.6 65.5 %reduce-scatter.2.cloned.1.call-done = f32[24,1536]{1,0:T(8,128)} async-done(((f32[768,1536]{1,0:T(8,128)}), f32[24,1536]{1,0:T(8,128)}) %reduce-scatter.2.cloned.1.call-update) | async-done | bytes 147472 | tf_op jit(solution)/shard_map/reduce_scatter | solution.py:133
  921.1 7.7 all_gather.43
  928.8 0.8 copy.27
  (76 shorter events, 1.2 us)
Async XLA Ops:
  7.2 41.5 %copy-start.17 = (bf16[256,768]{1,0:T(8,128)(2,1)S(1)}, bf16[256,768]{1,0:T(8,128)(2,1)}, u32[]{:S(2)}) copy-start(bf16[256,768]{1,0:T(8,128)(2,1)} %param.16) | copy-start | bytes 1179652
  7.2 41.5 %copy-start.23 = (s32[256]{0:T(256)S(1)}, s32[256]{0:T(256)}, u32[]{:S(2)}) copy-start(s32[256]{0:T(256)} %param.17) | copy-start | bytes 3076
  7.2 49.5 %all-gather.10.cloned.1.call-start = ((), (), s32[]{:S(2)}) async-start(), calls=%async_computation.1 | async-start | bytes 1327104 | tf_op jit(solution)/shard_map/all_gather | solution.py:66
  7.9 91.1 %all-gather.12.cloned.1.call-start = ((), (), s32[]{:S(2)}) async-start(), calls=%async_computation.2 | async-start | bytes 1327104 | tf_op jit(solution)/shard_map/all_gather | solution.py:71
  8.7 132.4 %all-gather.14.cloned.1.call-start = ((), (), s32[]{:S(2)}) async-start(), calls=%async_computation.3 | async-start | bytes 1327104 | tf_op jit(solution)/shard_map/all_gather | solution.py:67
  9.4 198.3 %all-gather.18.cloned.1.call-start = ((), (), s32[]{:S(2)}) async-start(), calls=%async_computation.6 | async-start | bytes 3981312 | tf_op jit(solution)/shard_map/all_gather | solution.py:73
  10.0 327.2 %all-reduce.5.cloned.1.call-start = ((), (), s32[]{:S(2)}) async-start(), calls=%async_computation.4 | async-start | bytes 393216 | tf_op jit(solution)/shard_map/psum | solution.py:98
  47.7 1.0 copy-start.2
  49.1 49.9 %copy-start.8 = (f32[64,768]{1,0:T(8,128)S(1)}, f32[64,768]{1,0:T(8,128)}, u32[]{:S(2)}) copy-start(f32[64,768]{1,0:T(8,128)} %param.22) | copy-start | bytes 589828
  58.5 349.6 %copy-start.5 = (bf16[256,768]{1,0:T(8,128)(2,1)}, bf16[256,768]{1,0:T(8,128)(2,1)S(1)}, u32[]{:S(2)}) copy-start(bf16[256,768]{1,0:T(8,128)(2,1)S(1)} %convolution_convert_fusion.1) | copy-start | bytes 1179652
  142.8 266.8 %copy-start.4 = (bf16[256,768]{1,0:T(8,128)(2,1)}, bf16[256,768]{1,0:T(8,128)(2,1)S(1)}, u32[]{:S(2)}) copy-start(bf16[256,768]{1,0:T(8,128)(2,1)S(1)} %convolution_convert_fusion) | copy-start | bytes 1179652
  143.7 261.0 %all-gather.16.cloned.1.call-start = ((), (), s32[]{:S(2)}) async-start(), calls=%async_computation.5 | async-start | bytes 3981312 | tf_op jit(solution)/shard_map/all_gather | solution.py:72
  144.3 389.9 %all-reduce.7.cloned.1.call-start = ((), (), s32[]{:S(2)}) async-start(), calls=%async_computation.7 | async-start | bytes 393216 | tf_op jit(solution)/shard_map/psum | solution.py:98
  407.7 1.3 copy-start.1
  407.9 2.6 copy-start.9
  409.6 0.9 copy-start.15
  410.6 123.6 %copy-start = (bf16[768,2304]{1,0:T(8,128)(2,1)S(1)}, bf16[768,2304]{1,0:T(8,128)(2,1)}, u32[]{:S(2)}) copy-start(bf16[768,2304]{1,0:T(8,128)(2,1)} %all-gather.16.cloned.1.call-done) | copy-start | bytes 10616836
  410.6 257.9 %all-reduce.9.cloned.1.call-start = ((), (), s32[]{:S(2)}) async-start(), calls=%async_computation.8 | async-start | bytes 393216 | tf_op jit(solution)/shard_map/psum | solution.py:98
  410.6 3.8 copy-start.16
  534.2 1.8 copy-start.10
  534.2 1.8 copy-start.12
  536.2 0.7 copy-start.6
  537.1 7.6 copy-start.22
  540.7 4.0 copy-start.19
  542.7 170.0 %all-gather.22.cloned.1.call-start = ((), (), s32[]{:S(2)}) async-start(), calls=%async_computation.10 | async-start | bytes 1327104 | tf_op jit(solution)/shard_map/all_gather | solution.py:74
  543.4 211.2 %all-gather.20.cloned.1.call-start = ((), (), s32[]{:S(2)}) async-start(), calls=%async_computation.9 | async-start | bytes 1327104 | tf_op jit(solution)/shard_map/all_gather | solution.py:104
  544.0 263.3 %all-gather.24.cloned.1.call-start = ((), (), s32[]{:S(2)}) async-start(), calls=%async_computation.11 | async-start | bytes 2654208 | tf_op jit(solution)/shard_map/all_gather | solution.py:116
  544.7 376.4 %reduce-scatter.2.cloned.1.call-start = ((), (), s32[]{:S(2)}) async-start(), calls=%async_computation.12 | async-start | bytes 4866048 | tf_op jit(solution)/shard_map/reduce_scatter | solution.py:133
  572.6 2.6 copy-start.14
  572.6 2.6 copy-start.20
  668.4 1.8 copy-start.7
  668.4 1.8 copy-start.11
  670.2 84.3 %copy-start.3 = (f32[256,768]{1,0:T(8,128)S(1)}, f32[256,768]{1,0:T(8,128)}, u32[]{:S(2)}) copy-start(f32[256,768]{1,0:T(8,128)} %convolution_add_fusion) | copy-start | bytes 2359300
  670.4 86.2 %copy-start.13 = (f32[64,768]{1,0:T(8,128)}, f32[64,768]{1,0:T(8,128)S(1)}, u32[]{:S(2)}) copy-start(f32[64,768]{1,0:T(8,128)S(1)} %fusion.23) | copy-start | bytes 589828
  756.9 52.9 %copy-start.18 = (bf16[1536,3]{0,1:T(4,128)(2,1)S(1)}, bf16[1536,3]{0,1:T(4,128)(2,1)}, u32[]{:S(2)}) copy-start(bf16[1536,3]{0,1:T(4,128)(2,1)} %reshape.72) | copy-start | bytes 27652
  756.9 52.9 %copy-start.21 = (f32[3,256]{1,0:T(4,128)S(1)}, f32[3,256]{1,0:T(4,128)}, u32[]{:S(2)}) copy-start(f32[3,256]{1,0:T(4,128)} %param.20) | copy-start | bytes 9220
Sparse Core Ops, SparseCore 0:
  10.2 46.4 all-gather.9
  58.9 40.0 all-gather.11
  101.2 39.7 all-gather.13
  143.1 64.5 all-gather.17
  213.7 123.4 all-reduce.4
  339.2 65.5 all-gather.15
  410.7 123.4 all-reduce.6
  542.8 125.5 all-reduce.8
  670.6 42.0 all-gather.21
  714.7 39.7 all-gather.19
  756.7 50.4 all-gather.23
  815.0 106.0 reduce-scatter.1
where the time goes:
time: 938 us
  waiting for transfers between devices  640 us (68%)
  blocking collectives  228 us (24%)
  matrix products  43.8 us (5%)
  between operations  16.3 us (2%)
    psum x3, waiting for transfers between devices, on_device(): numer, denom = lax.psum((numer, denom), ('tok', 'rep'))  258 us
    psum x3, blocking collectives, on_device(): numer, denom = lax.psum((numer, denom), ('tok', 'rep'))  118 us
    all_gather x1, waiting for transfers between devices, on_device(): lax.all_gather(gru_input, 'tok', axis=0, tiled=True)  67.6 us
    reduce_scatter x1, waiting for transfers between devices, on_device(): lax.psum_scatter(lax.dot_general(joined, dpre, (((0,), (0,)), ((), ())),...  65.5 us
    all_gather x1, waiting for transfers between devices, on_device(): pre = add_rows(joined, lax.all_gather(render_in, 'tok', axis=0, tiled=True))  50.4 us
    all_gather x1, waiting for transfers between devices, on_device(): lax.all_gather(mix_key, 'tok', axis=0, tiled=True)  42.3 us
    all_gather x1, waiting for transfers between devices, on_device(): lax.all_gather(query_weight, 'tok', axis=0, tiled=True)  40.5 us
    all_gather x1, waiting for transfers between devices, on_device(): lax.all_gather(mix_query, 'tok', axis=0, tiled=True)  40.3 us
  transfers between devices with their start and end apart: 12, of which 12 were waited for; matrix products, arithmetic and copies ran while one was open for 3% of the time, Pallas kernels for 0%

commit v1 on v0

v1 whole, which is shorter than its diff:
```python
import jax
import jax.numpy as jnp
from jax import lax
from jax.sharding import PartitionSpec as P

ITERS = 3


EPSILON = 1e-05
ATTN_FLOOR = 1e-08
BOTH = ("tok", "rep")
F32 = jnp.float32
BF16 = jnp.bfloat16


def normalize(values):
    mean = jnp.mean(values, axis=-1, keepdims=True)
    centred = values - mean
    spread = jnp.mean(centred * centred, axis=-1, keepdims=True)
    return centred * lax.rsqrt(spread + EPSILON)


def dot(left, right, left_dim=1, right_dim=0):
    return lax.dot_general(
        left, right, (((left_dim,), (right_dim,)), ((), ())), preferred_element_type=F32
    )


def lookup(table, index):
    onehot = (index[:, None] == jnp.arange(table.shape[0], dtype=jnp.int32)[None, :]).astype(BF16)
    return dot(onehot, table)


def chunk_shape(shape, parts):
    rows, width = shape
    if rows % parts == 0:
        return (rows // parts, width)
    return (1, rows * width // parts)


def spread_out(chunk, axis):
    copies = lax.axis_size(axis)
    return lax.all_to_all(jnp.broadcast_to(chunk[None], (copies,) + chunk.shape), axis, 0, 0)


def sum_chunks(whole, axis, extra=None):
    copies = lax.axis_size(axis)
    pieces = whole.astype(BF16).reshape((copies,) + chunk_shape(whole.shape, copies))
    if extra is not None:
        extra = jnp.broadcast_to(extra.astype(BF16)[None], (copies,) + extra.shape)
        pieces = jnp.concatenate([pieces, extra], axis=1)
    return jnp.sum(lax.all_to_all(pieces, axis, 0, 0).astype(F32), axis=0)


def gru(slots, update, gru_input, gru_hidden):
    width = slots.shape[1]
    from_update = dot(update, gru_input)
    from_state = dot(slots.astype(BF16), gru_hidden)
    reset = jax.nn.sigmoid(from_update[:, :width] + from_state[:, :width])
    blend = jax.nn.sigmoid(from_update[:, width : 2 * width] + from_state[:, width : 2 * width])
    candidate = jnp.tanh(from_update[:, 2 * width :] + reset * from_state[:, 2 * width :])
    return (1.0 - blend) * candidate + blend * slots


def on_device(
    patches,
    patch_view,
    rays,
    ray_view,
    targets,
    camera,
    slots_init,
    key_weight,
    value_weight,
    query_weight,
    gru_input,
    gru_hidden,
    mix_query,
    mix_key,
    render_in,
    render_out,
):
    width = patches.shape[1]
    scale = width ** (-0.5)
    slot_count = slots_init.shape[0]
    toks, reps = lax.axis_size("tok"), lax.axis_size("rep")
    parts = toks * reps
    rep = lax.axis_index("rep")
    me = lax.axis_index("tok") * reps + rep

    def piece(rows):
        size = rows.shape[0] // reps
        return lax.dynamic_slice_in_dim(rows, rep * size, size, 0)

    key_piece, query_piece = piece(key_weight), piece(query_weight)
    first = jnp.concatenate(
        [key_piece, piece(value_weight), query_piece, piece(gru_input), piece(gru_hidden)], axis=1
    )
    first = lax.all_gather(first, BOTH, axis=0, tiled=True)
    second = jnp.concatenate([piece(mix_query), piece(mix_key), piece(render_in)], axis=1)

    camera_piece = piece(camera)
    rows = camera_piece.shape[0]
    table = spread_out(camera_piece, "tok").reshape(toks * rows, width)
    table = lax.all_gather(table, "rep", axis=0, tiled=True)

    def place(view):
        of_tok, of_rep = view // (rows * reps), (view // rows) % reps
        return (of_rep * toks + of_tok) * rows + view % rows

    start = normalize(slots_init).astype(BF16)
    depth = query_piece.shape[0]
    query_part = dot(lax.dynamic_slice_in_dim(start, me * depth, depth, 1), query_piece)
    query_chunk = (sum_chunks(query_part, BOTH) * scale).astype(BF16)
    colours = render_out.shape[0]
    flat = render_out.reshape(-1)
    lanes = query_chunk.shape[1]
    extra_rows = -(-flat.shape[0] // lanes)
    flat = jnp.pad(flat, (0, extra_rows * lanes - flat.shape[0])).reshape(extra_rows, lanes)
    got = spread_out(jnp.concatenate([query_chunk, flat], axis=0), BOTH)
    query = got[:, : query_chunk.shape[0]].reshape(slot_count, width)
    colour_full = got[:, query_chunk.shape[0] :].reshape(toks, reps, -1)[:, 0, : render_out.size]
    colour_full = colour_full.reshape(toks, colours, -1).transpose(1, 0, 2).reshape(colours, -1)
    reach = spread_out(dot(key_piece, query, 1, 1).astype(BF16), BOTH).reshape(width, slot_count)

    patch_x = normalize(patches.astype(F32) + lookup(table, place(patch_view))).astype(BF16)

    def gather_update(logits, source):
        attn = jax.nn.softmax(logits, axis=1) + ATTN_FLOOR
        numer = dot(attn.astype(BF16), source, 0, 0)
        denom = jnp.sum(attn, axis=0)
        chunk = chunk_shape(numer.shape, parts)
        denom = jnp.pad(denom, (0, -slot_count % chunk[1])).reshape(-1, chunk[1])
        total = sum_chunks(numer, BOTH, denom)
        denom = total[chunk[0] :].reshape(-1)[:slot_count]
        slot_of = (me * chunk[0] * chunk[1] + jnp.arange(chunk[0] * chunk[1])) // width
        slot_of = slot_of.reshape(chunk)[:, :1]
        mine = jnp.sum(jnp.where(slot_of == jnp.arange(slot_count)[None, :], denom[None, :], 0.0), axis=1)
        part = (total[: chunk[0]] / mine[:, None]).astype(BF16)
        return spread_out(part, BOTH).reshape(slot_count, width)

    seen = gather_update(dot(patch_x, reach), patch_x)

    ray_rows = rays.shape[0]
    half = ray_rows // 2
    group = jnp.concatenate(
        [
            lax.all_gather(rays[:half], "rep", axis=0),
            lax.all_gather(rays[half:], "rep", axis=0),
        ],
        axis=1,
    ).reshape(reps * ray_rows, width)
    aside = jnp.concatenate([targets, ray_view.astype(F32)[None]], axis=0)
    aside = lax.all_gather(aside, "rep", axis=1, tiled=True)
    group_targets, group_view = aside[:colours], aside[colours].astype(jnp.int32)
    ray_in = group.astype(F32) + lookup(table, place(group_view))
    ray_x = ray_in.astype(BF16)

    keys = dot(patch_x, first[:, :width]).astype(BF16)
    value_full = first[:, width : 2 * width]
    values = dot(patch_x, value_full).astype(BF16)
    reached = (dot(keys, first[:, 2 * width : 3 * width], 1, 1) * scale).astype(BF16)
    input_full = first[:, 3 * width : 6 * width]
    hidden_full = first[:, 6 * width :]
    second = lax.all_gather(second, BOTH, axis=0, tiled=True)

    slots = gru(slots_init, dot(seen, value_full).astype(BF16), input_full, hidden_full)
    for step in range(1, ITERS):
        logits = dot(reached, normalize(slots).astype(BF16), 1, 1)
        slots = gru(slots, gather_update(logits, values), input_full, hidden_full)

    slots_low = slots.astype(BF16)
    slot_keys = dot(slots_low, second[:, width : 2 * width]).astype(BF16)
    mixer = (dot(second[:, :width], slot_keys, 1, 1) * scale).astype(BF16)
    mix = jax.nn.softmax(dot(ray_x, mixer), axis=1).astype(BF16)
    joined = (dot(mix, slots_low) + ray_in).astype(BF16)

    units = render_in.shape[1] // reps
    head = lax.dynamic_slice_in_dim(second, 2 * width + rep * units, units, 1)
    colour_head = lax.dynamic_slice_in_dim(colour_full, rep * units, units, 1)
    pre = dot(joined, head)
    sig = jax.nn.sigmoid(pre)
    hidden = (pre * sig).astype(BF16)
    colour = jnp.sum(lax.all_gather(dot(colour_head, hidden, 1, 1), "rep", axis=0), axis=0)
    error = colour - group_targets
    rays_total = ray_rows * parts
    dcol = (error * (2.0 / jnp.sqrt(jnp.float32(3.0 * rays_total)))).astype(BF16)
    squared = jnp.sum(error * error)
    out_part = dot(dcol, hidden)
    dhidden = dot(dcol, colour_head, 0, 0)
    dpre = (dhidden * (sig + pre * sig * (1.0 - sig))).astype(BF16)
    grad = dot(joined, dpre, 0, 0)
    below = jnp.concatenate([out_part, jnp.broadcast_to(squared, (1, units))], axis=0)
    total = sum_chunks(grad, "tok", below)
    total = lax.all_gather(total, "rep", axis=1, tiled=True)
    mine = width // toks
    return (
        slots,
        lax.dynamic_slice_in_dim(colour, rep * ray_rows, ray_rows, 1),
        total[mine + colours, 0] / (3.0 * rays_total),
        total[:mine],
        total[mine : mine + colours],
    )


def solution(mesh):
    placed = (
        P(("tok", "rep"), None),
        P(("tok", "rep")),
        P(("tok", "rep"), None),
        P(("tok", "rep")),
        P(None, ("tok", "rep")),
        P("tok", None),
        P(),
        P("tok", None),
        P("tok", None),
        P("tok", None),
        P("tok", None),
        P("tok", None),
        P("tok", None),
        P("tok", None),
        P("tok", None),
        P(None, "tok"),
    )
    return jax.shard_map(
        on_device,
        mesh=mesh,
        in_specs=placed,
        out_specs=(P(), P(None, ("tok", "rep")), P(), P("tok", None), P()),
        check_vma=False,
    )
```

time: 938 us -> 257 us (0.27)
  waiting for transfers between devices: 640 us -> 76.5 us
  blocking collectives: 228 us -> 50.2 us
  starting transfers between devices: 0.47 us -> 42.9 us
  local copies, waits for them, and re-layouts: 4.09 us -> 16.6 us
    all_gather x8 -> x2, waiting for transfers between devices: 312 us -> 0.04 us  [the longest x1 0.02 us: on_device(): first = lax.all_gather(first, BOTH, axis=0, tiled=True)]
    psum x3 -> x0, waiting for transfers between devices: 258 us -> none  [on_device(): numer, denom = lax.psum((numer, denom), ('tok', 'rep'))]
    psum x4 -> x0, blocking collectives: 157 us -> none  [the longest x3 118 us: on_device(): numer, denom = lax.psum((numer, denom), ('tok', 'rep'))]
    all_to_all x0 -> x11, waiting for transfers between devices: none -> 76.5 us  [the longest x5 38.4 us: sum_chunks(): return jnp.sum(lax.all_to_all(pieces, axis, 0, 0).astype(F32), axis=0)]
    reduce_scatter x1 -> x0, waiting for transfers between devices: 65.5 us -> none  [on_device(): lax.psum_scatter(lax.dot_general(joined, dpre, (((0,), (0,)), ((), ())),...]
    all_to_all x0 -> x11, starting transfers between devices: none -> 42.8 us  [the longest x6 24 us: spread_out(): lax.all_to_all(jnp.broadcast_to(chunk[None], (copies,) + chunk.shape), ax...]
    all_gather x3 -> x6, blocking collectives: 70.3 us -> 50.2 us  [the longest x1 13 us: on_device(): table = lax.all_gather(table, 'rep', axis=0, tiled=True)]
    dot_general x23 -> x25, matrix products: 43.8 us -> 40.5 us  [dot(): lax.dot_general(left, right, (((left_dim,), (right_dim,)), ((), ())), pre...]
  transfers between devices with their start and end apart: 12 -> 13, of which waited for: 12 -> 9; matrix products, arithmetic and copies ran while one was open for 3% -> 19% of each run, Pallas kernels for 0% -> 0%
where the time goes in v1:
time: 257 us; the launch traced here: 255 us
  waiting for transfers between devices  76.5 us (30%)
  blocking collectives  50.2 us (20%)
  starting transfers between devices  42.9 us (17%)
  matrix products  40.5 us (16%)
  local copies, waits for them, and re-layouts  16.6 us (6%)
  between operations  16.5 us (6%)
  other arithmetic  12 us (5%)
    dot_general x25, matrix products, dot(): lax.dot_general(left, right, (((left_dim,), (right_dim,)), ((), ())), pre...  40.5 us
    all_to_all x5, waiting for transfers between devices, sum_chunks(): return jnp.sum(lax.all_to_all(pieces, axis, 0, 0).astype(F32), axis=0)  38.4 us
    all_to_all x6, waiting for transfers between devices, spread_out(): lax.all_to_all(jnp.broadcast_to(chunk[None], (copies,) + chunk.shape), ax...  38 us
    all_to_all x6, starting transfers between devices, spread_out(): lax.all_to_all(jnp.broadcast_to(chunk[None], (copies,) + chunk.shape), ax...  24 us
    all_to_all x5, starting transfers between devices, sum_chunks(): return jnp.sum(lax.all_to_all(pieces, axis, 0, 0).astype(F32), axis=0)  18.8 us
    all_gather x1, blocking collectives, on_device(): table = lax.all_gather(table, 'rep', axis=0, tiled=True)  13 us
    all_gather x1, blocking collectives, on_device(): lax.all_gather(rays[half:], 'rep', axis=0)  10.2 us
    all_gather x1, blocking collectives, on_device(): lax.all_gather(rays[:half], 'rep', axis=0)  9.32 us
  transfers between devices with their start and end apart: 13, of which 9 were waited for; matrix products, arithmetic and copies ran while one was open for 19% of the time, Pallas kernels for 0%

profile of v1, /device:TPU:0, one launch (start us, length us, event | category | flops | bytes accessed | tf_op | source)
XLA Modules:
  0.0 255.2 jit_solution(45933608014107696)
XLA Ops:
  7.3 0.9 dynamic-slice_dynamic-update-slice_fusion.4
  8.1 0.8 dynamic-slice_dynamic-update-slice_fusion.2
  8.9 0.8 dynamic-slice_dynamic-update-slice_fusion.3
  9.7 0.9 dynamic-slice_dynamic-update-slice_fusion.1
  10.6 0.9 dynamic-slice_dynamic-update-slice_fusion
  11.5 0.7 copy-done.10
  12.3 1.0 reduce_sum.227
  13.3 1.1 multiply_reduce_fusion.3
  14.5 1.0 convolution_convert_fusion.7
  16.1 7.3 %all-to-all-start.1 = ((bf16[32,2,768]{2,1,0:T(2,128)(2,1)}), bf16[32,2,768]{2,1,0:T(2,128)(2,1)S(1)}, u32[]{:S(2)}, u32[]{:S(2)}) async-start(bf16[32,2,768]{2,1,0:T(2,128)(2,1)} %reshape.216), calls=%async_computation.1 | async-start | bytes 196608 | tf_op jit(solution)/shard_map/all_to_all | solution.py:52
  23.5 0.8 constant_dynamic-slice_fusion.2
  25.2 5.3 %all_gather.39 = f32[4,1024]{1,0:T(4,128)S(1)} all-gather(f32[4,256]{1,0:T(4,128)S(1)} %pad_maximum_fusion.7), channel_id=1, replica_groups=mesh['tok'=8,'rep'=4] {'rep'}, dimensions={1}, use_global_device_ids=true | all-gather | bytes 20480 | tf_op jit(solution)/shard_map/all_gather | solution.py:154
  30.6 9.3 %all-gather = bf16[512,768]{1,0:T(8,128)(2,1)} all-gather(bf16[128,768]{1,0:T(8,128)(2,1)S(1)} %get-tuple-element.11), channel_id=2, replica_groups=mesh['tok'=8,'rep'=4] {'rep'}, dimensions={0}, use_global_device_ids=true | all-gather | bytes 983040 | tf_op jit(solution)/shard_map/all_gather | solution.py:148
  39.9 0.7 constant_dynamic-slice_fusion.5
  40.8 0.7 broadcast_in_dim.52
  41.5 5.7 %all-to-all-start = ((bf16[8,16,768]{2,1,0:T(8,128)(2,1)}), bf16[8,16,768]{2,1,0:T(8,128)(2,1)S(1)}, u32[]{:S(2)}, u32[]{:S(2)}) async-start(bf16[8,16,768]{2,1,0:T(8,128)(2,1)} %broadcast_in_dim.52), calls=%async_computation | async-start | bytes 393216 | tf_op jit(solution)/shard_map/all_to_all | solution.py:43
  47.3 13.4 %all-to-all-done = bf16[8,16,768]{2,1,0:T(8,128)(2,1)S(1)} async-done(((bf16[8,16,768]{2,1,0:T(8,128)(2,1)}), bf16[8,16,768]{2,1,0:T(8,128)(2,1)S(1)}, u32[]{:S(2)}, u32[]{:S(2)}) %all-to-all-start) | async-done | bytes 196640 | tf_op jit(solution)/shard_map/all_to_all | solution.py:43
  60.7 0.7 broadcast_in_dim.53
  61.4 3.8 %all-to-all-start.2 = ((bf16[32,3,768]{2,1,0:T(4,128)(2,1)}), bf16[32,3,768]{2,1,0:T(4,128)(2,1)S(1)}, u32[]{:S(2)}, u32[]{:S(2)}) async-start(bf16[32,3,768]{2,1,0:T(4,128)(2,1)} %broadcast_in_dim.53), calls=%async_computation.2 | async-start | bytes 393216 | tf_op jit(solution)/shard_map/all_to_all | solution.py:43
  65.2 13.0 %all_gather.33 = bf16[512,768]{1,0:T(8,128)(2,1)S(1)} all-gather(bf16[128,768]{1,0:T(8,128)(2,1)S(1)} %bitcast.48), channel_id=1, replica_groups=mesh['tok'=8,'rep'=4] {'rep'}, dimensions={0}, use_global_device_ids=true | all-gather | bytes 983040 | tf_op jit(solution)/shard_map/all_gather | solution.py:105
  79.2 0.9 convolution_convert_fusion.8
  80.1 0.8 reshape.240
  80.9 5.0 %all-to-all-start.3 = ((bf16[32,2,768]{2,1,0:T(2,128)(2,1)}), bf16[32,2,768]{2,1,0:T(2,128)(2,1)S(1)}, u32[]{:S(2)}, u32[]{:S(2)}) async-start(bf16[32,2,768]{2,1,0:T(2,128)(2,1)} %reshape.240), calls=%async_computation.3 | async-start | bytes 196608 | tf_op jit(solution)/shard_map/all_to_all | solution.py:43
  86.1 7.6 %all-to-all-done.3 = bf16[32,2,768]{2,1,0:T(2,128)(2,1)S(1)} async-done(((bf16[32,2,768]{2,1,0:T(2,128)(2,1)}), bf16[32,2,768]{2,1,0:T(2,128)(2,1)S(1)}, u32[]{:S(2)}, u32[]{:S(2)}) %all-to-all-start.3) | async-done | bytes 98336 | tf_op jit(solution)/shard_map/all_to_all | solution.py:43
  94.7 0.9 pad_maximum_fusion.2
  95.6 2.6 %all-to-all-start.4 = ((bf16[32,3,768]{2,1,0:T(4,128)(2,1)}), bf16[32,3,768]{2,1,0:T(4,128)(2,1)S(1)}, u32[]{:S(2)}, u32[]{:S(2)}) async-start(bf16[32,3,768]{2,1,0:T(4,128)(2,1)} %pad_maximum_fusion.2), calls=%async_computation.4 | async-start | bytes 393216 | tf_op jit(solution)/shard_map/all_to_all | solution.py:52
  98.2 10.2 %all-gather.1 = bf16[512,768]{1,0:T(8,128)(2,1)} all-gather(bf16[128,768]{1,0:T(8,128)(2,1)S(1)} %get-tuple-element.12), channel_id=3, replica_groups=mesh['tok'=8,'rep'=4] {'rep'}, dimensions={0}, use_global_device_ids=true | all-gather | bytes 983040 | tf_op jit(solution)/shard_map/all_gather | solution.py:149
  108.4 3.0 %all-to-all-done.4 = bf16[32,3,768]{2,1,0:T(4,128)(2,1)S(1)} async-done(((bf16[32,3,768]{2,1,0:T(4,128)(2,1)}), bf16[32,3,768]{2,1,0:T(4,128)(2,1)S(1)}, u32[]{:S(2)}, u32[]{:S(2)}) %all-to-all-start.4) | async-done | bytes 147488 | tf_op jit(solution)/shard_map/all_to_all | solution.py:52
  111.8 0.7 broadcast_in_dim.59
  112.5 3.1 %all-to-all-start.5 = ((bf16[32,2,768]{2,1,0:T(2,128)(2,1)}), bf16[32,2,768]{2,1,0:T(2,128)(2,1)S(1)}, u32[]{:S(2)}, u32[]{:S(2)}) async-start(bf16[32,2,768]{2,1,0:T(2,128)(2,1)} %broadcast_in_dim.59), calls=%async_computation.5 | async-start | bytes 196608 | tf_op jit(solution)/shard_map/all_to_all | solution.py:43
  115.6 7.8 %all-to-all-done.5 = bf16[32,2,768]{2,1,0:T(2,128)(2,1)S(1)} async-done(((bf16[32,2,768]{2,1,0:T(2,128)(2,1)}), bf16[32,2,768]{2,1,0:T(2,128)(2,1)S(1)}, u32[]{:S(2)}, u32[]{:S(2)}) %all-to-all-start.5) | async-done | bytes 98336 | tf_op jit(solution)/shard_map/all_to_all | solution.py:43
  123.5 2.8 %convolution_bitcast_fusion = f32[64,2304]{1,0:T(8,128)S(1)} fusion(bf16[768,6912]{1,0:T(8,128)(2,1)} %all-gather.7.cloned.1.call-done, f32[64,768]{1,0:T(8,128)S(1)} %copy-done.2), kind=kOutput, calls=%fused_computation | convolution fusion | flops 226541568 | bytes 4325376 | tf_op jit(solution)/shard_map/dot_general | solution.py:24
  126.3 3.4 %fusion.9 = f32[64,2304]{1,0:T(8,128)S(1)} fusion(bf16[768,6912]{1,0:T(8,128)(2,1)} %all-gather.7.cloned.1.call-done, bf16[64,768]{1,0:T(8,128)(2,1)S(1)} %reshape.222), kind=kOutput, calls=%fused_computation.12 | convolution fusion | flops 302039040 | bytes 5406720 | tf_op jit(solution)/shard_map/dot_general | solution.py:24
  130.1 2.5 fusion.15
  133.0 1.8 convolution_convert_fusion.1
  135.2 0.9 pad_maximum_fusion.3
  136.1 2.6 %all-to-all-start.6 = ((bf16[32,3,768]{2,1,0:T(4,128)(2,1)}), bf16[32,3,768]{2,1,0:T(4,128)(2,1)S(1)}, u32[]{:S(2)}, u32[]{:S(2)}) async-start(bf16[32,3,768]{2,1,0:T(4,128)(2,1)} %pad_maximum_fusion.3), calls=%async_computation.6 | async-start | bytes 393216 | tf_op jit(solution)/shard_map/all_to_all | solution.py:52
  138.7 1.5 pad_maximum_fusion
  140.2 9.3 %all-to-all-done.6 = bf16[32,3,768]{2,1,0:T(4,128)(2,1)S(1)} async-done(((bf16[32,3,768]{2,1,0:T(4,128)(2,1)}), bf16[32,3,768]{2,1,0:T(4,128)(2,1)S(1)}, u32[]{:S(2)}, u32[]{:S(2)}) %all-to-all-start.6) | async-done | bytes 147488 | tf_op jit(solution)/shard_map/all_to_all | solution.py:52
  149.9 0.7 broadcast_in_dim.63
  150.6 3.2 %all-to-all-start.7 = ((bf16[32,2,768]{2,1,0:T(2,128)(2,1)}), bf16[32,2,768]{2,1,0:T(2,128)(2,1)S(1)}, u32[]{:S(2)}, u32[]{:S(2)}) async-start(bf16[32,2,768]{2,1,0:T(2,128)(2,1)} %broadcast_in_dim.63), calls=%async_computation.7 | async-start | bytes 196608 | tf_op jit(solution)/shard_map/all_to_all | solution.py:43
  153.8 3.6 %fusion.2 = f32[64,2304]{1,0:T(8,128)} fusion(bf16[768,6912]{1,0:T(8,128)(2,1)} %all-gather.7.cloned.1.call-done, f32[64,768]{1,0:T(8,128)S(1)} %get-tuple-element.8), kind=kOutput, calls=%fused_computation.5 | convolution fusion | flops 226541568 | bytes 4325376 | tf_op jit(solution)/shard_map/dot_general | solution.py:24
  157.4 4.2 %all-to-all-done.7 = bf16[32,2,768]{2,1,0:T(2,128)(2,1)S(1)} async-done(((bf16[32,2,768]{2,1,0:T(2,128)(2,1)}), bf16[32,2,768]{2,1,0:T(2,128)(2,1)S(1)}, u32[]{:S(2)}, u32[]{:S(2)}) %all-to-all-start.7) | async-done | bytes 98336 | tf_op jit(solution)/shard_map/all_to_all | solution.py:43
  161.6 2.8 %fusion.7 = f32[64,2304]{1,0:T(8,128)S(1)} fusion(bf16[64,768]{1,0:T(8,128)(2,1)S(1)} %reshape.224, bf16[768,6912]{1,0:T(8,128)(2,1)} %all-gather.7.cloned.1.call-done), kind=kOutput, calls=%fused_computation.10 | convolution fusion | flops 226492416 | bytes 4227072 | tf_op jit(solution)/shard_map/dot_general | solution.py:24
  165.9 0.9 pad_maximum_fusion.4
  166.8 2.8 %all-to-all-start.8 = ((bf16[32,3,768]{2,1,0:T(4,128)(2,1)}), bf16[32,3,768]{2,1,0:T(4,128)(2,1)S(1)}, u32[]{:S(2)}, u32[]{:S(2)}) async-start(bf16[32,3,768]{2,1,0:T(4,128)(2,1)} %pad_maximum_fusion.4), calls=%async_computation.8 | async-start | bytes 393216 | tf_op jit(solution)/shard_map/all_to_all | solution.py:52
  169.6 2.7 %fusion.12 = f32[1024,768]{1,0:T(8,128)} fusion(bf16[512,768]{1,0:T(8,128)(2,1)S(1)} %all_gather.33, s32[1024]{0:T(1024)S(1)} %fusion.119), kind=kOutput, calls=%fused_computation.16 | convolution fusion | flops 805830656 | bytes 3936256 | tf_op jit(solution)/shard_map/dot_general | solution.py:24
  172.9 9.1 %all-to-all-done.8 = bf16[32,3,768]{2,1,0:T(4,128)(2,1)S(1)} async-done(((bf16[32,3,768]{2,1,0:T(4,128)(2,1)}), bf16[32,3,768]{2,1,0:T(4,128)(2,1)S(1)}, u32[]{:S(2)}, u32[]{:S(2)}) %all-to-all-start.8) | async-done | bytes 147488 | tf_op jit(solution)/shard_map/all_to_all | solution.py:52
  182.3 0.7 broadcast_in_dim.67
  183.0 3.2 %all-to-all-start.9 = ((bf16[32,2,768]{2,1,0:T(2,128)(2,1)}), bf16[32,2,768]{2,1,0:T(2,128)(2,1)S(1)}, u32[]{:S(2)}, u32[]{:S(2)}) async-start(bf16[32,2,768]{2,1,0:T(2,128)(2,1)} %broadcast_in_dim.67), calls=%async_computation.9 | async-start | bytes 196608 | tf_op jit(solution)/shard_map/all_to_all | solution.py:43
  186.2 2.7 %fusion = f32[64,2304]{1,0:T(8,128)S(1)} fusion(bf16[768,6912]{1,0:T(8,128)(2,1)} %all-gather.7.cloned.1.call-done, f32[64,768]{1,0:T(8,128)S(1)} %get-tuple-element.6), kind=kOutput, calls=%fused_computation.3 | convolution fusion | flops 226541568 | bytes 4325376 | tf_op jit(solution)/shard_map/dot_general | solution.py:24
  189.0 5.0 %all-to-all-done.9 = bf16[32,2,768]{2,1,0:T(2,128)(2,1)S(1)} async-done(((bf16[32,2,768]{2,1,0:T(2,128)(2,1)}), bf16[32,2,768]{2,1,0:T(2,128)(2,1)S(1)}, u32[]{:S(2)}, u32[]{:S(2)}) %all-to-all-start.9) | async-done | bytes 98336 | tf_op jit(solution)/shard_map/all_to_all | solution.py:43
  194.0 2.7 %fusion.5 = f32[64,2304]{1,0:T(8,128)S(1)} fusion(bf16[64,768]{1,0:T(8,128)(2,1)S(1)} %reshape.226, bf16[768,6912]{1,0:T(8,128)(2,1)} %all-gather.7.cloned.1.call-done), kind=kOutput, calls=%fused_computation.8 | convolution fusion | flops 226492416 | bytes 4227072 | tf_op jit(solution)/shard_map/dot_general | solution.py:24
  197.0 2.4 fusion.32
  199.4 2.7 %fusion.147 = (f32[1024]{0:T(1024)S(1)}, f32[1024,64]{0,1:T(8,128)S(1)}) fusion(bf16[768,64]{0,1:T(8,128)(2,1)S(1)} %fusion.32, f32[1024,768]{1,0:T(8,128)} %fusion.12, bf16[1024,768]{1,0:T(8,128)(2,1)S(1)} %bitcast.43), kind=kOutput, calls=%fused_computation.250 | convolution fusion | flops 103087104 | bytes 5083136 | tf_op jit(solution)/shard_map/dot_general | solution.py:24
  202.2 0.7 add_convert_fusion
  202.9 2.7 %fusion.38 = (bf16[1024,384]{1,0:T(8,128)(2,1)S(1)}, f32[1024,384]{1,0:T(8,128)S(1)}) fusion(bf16[1024,768]{1,0:T(8,128)(2,1)S(1)} %add_convert_fusion, bf16[768,3072]{1,0:T(8,128)(2,1)} %all-gather.9.cloned.1.call-done, s32[]{:T(128)S(6)} %select_n.112), kind=kOutput, calls=%fused_computation.46 | convolution fusion | flops 605945856 | bytes 4521988 | tf_op jit(solution)/shard_map/dot_general | solution.py:24
  205.9 5.2 %all-gather.3 = f32[4,3,1024]{2,1,0:T(4,128)S(1)} all-gather(f32[1,3,1024]{2,1,0:T(4,128)S(1)} %convolution_bitcast_fusion.1), channel_id=4, replica_groups=mesh['tok'=8,'rep'=4] {'rep'}, dimensions={0}, use_global_device_ids=true | all-gather | bytes 61440 | tf_op jit(solution)/shard_map/all_gather | solution.py:184
  212.0 2.7 %convolution_convert_fusion = bf16[768,384]{1,0:T(8,128)(2,1)S(1)} fusion(bf16[1024,768]{1,0:T(8,128)(2,1)} %copy-done.6, bf16[3,1024]{1,0:T(4,128)(2,1)S(1)} %get-tuple-element.14, f32[1024,384]{1,0:T(8,128)S(1)} %get-tuple-element.26, bf16[3,1536]{1,0:T(4,128)(2,1)S(1)} %reshape.228, s32[]{:T(128)S(6)} %select_n.107), kind=kOutput, calls=%fused_computation.21 | convolution fusion | flops 610172928 | bytes 3746820 | tf_op jit(solution)/shard_map/dot_general | solution.py:24
  215.4 0.9 pad_maximum_fusion.1
  216.3 3.5 %all-to-all-start.10 = ((bf16[8,100,384]{2,1,0:T(8,128)(2,1)}), bf16[8,100,384]{2,1,0:T(8,128)(2,1)S(1)}, u32[]{:S(2)}, u32[]{:S(2)}) async-start(bf16[8,100,384]{2,1,0:T(8,128)(2,1)} %pad_maximum_fusion.1), calls=%async_computation.10 | async-start | bytes 1277952 | tf_op jit(solution)/shard_map/all_to_all | solution.py:52
  220.4 17.1 %all-to-all-done.10 = bf16[8,100,384]{2,1,0:T(8,128)(2,1)S(1)} async-done(((bf16[8,100,384]{2,1,0:T(8,128)(2,1)}), bf16[8,100,384]{2,1,0:T(8,128)(2,1)S(1)}, u32[]{:S(2)}, u32[]{:S(2)}) %all-to-all-start.10) | async-done | bytes 614432 | tf_op jit(solution)/shard_map/all_to_all | solution.py:52
  237.6 7.0 %all_gather.43 = f32[100,1536]{1,0:T(8,128)S(1)} all-gather(f32[100,384]{1,0:T(8,128)S(1)} %convert_reduce_fusion), channel_id=1, replica_groups=mesh['tok'=8,'rep'=4] {'rep'}, dimensions={1}, use_global_device_ids=true | all-gather | bytes 768000 | tf_op jit(solution)/shard_map/all_gather | solution.py:195
  244.6 0.9 slice.217
  (131 shorter events, 12.3 us)
Async XLA Ops:
  7.2 17.2 %copy-start = (bf16[96,1536]{1,0:T(8,128)(2,1)S(1)}, bf16[96,1536]{1,0:T(8,128)(2,1)}, u32[]{:S(2)}) copy-start(bf16[96,1536]{1,0:T(8,128)(2,1)} %param.30) | copy-start | bytes 884740
  7.2 17.9 %copy-start.14 = (bf16[3,192]{1,0:T(4,128)(2,1)S(1)}, bf16[3,192]{1,0:T(4,128)(2,1)}, u32[]{:S(2)}) copy-start(bf16[3,192]{1,0:T(4,128)(2,1)} %param.31) | copy-start | bytes 3460
  7.2 18.0 %copy-start.15 = (s32[256]{0:T(256)S(1)}, s32[256]{0:T(256)}, u32[]{:S(2)}) copy-start(s32[256]{0:T(256)} %param.19) | copy-start | bytes 3076
  7.2 18.0 %copy-start.13 = (f32[3,256]{1,0:T(4,128)S(1)}, f32[3,256]{1,0:T(4,128)}, u32[]{:S(2)}) copy-start(f32[3,256]{1,0:T(4,128)} %param.20) | copy-start | bytes 9220
  7.2 23.3 %copy-start.11 = (bf16[256,768]{1,0:T(8,128)(2,1)S(1)}, bf16[256,768]{1,0:T(8,128)(2,1)}, u32[]{:S(2)}) copy-start(bf16[256,768]{1,0:T(8,128)(2,1)} %param.18) | copy-start | bytes 1179652
  7.2 116.2 %all-gather.7.cloned.1.call-start = ((), (), s32[]{:S(2)}) async-start(), calls=%async_computation.11 | async-start | bytes 10948608 | tf_op jit(solution)/shard_map/all_gather | solution.py:99
  11.5 0.7 copy-start.10
  11.5 29.3 %copy-start.16 = (s32[256]{0:T(256)S(1)}, s32[256]{0:T(256)}, u32[]{:S(2)}) copy-start(s32[256]{0:T(256)} %param.17) | copy-start | bytes 3076
  16.1 24.7 %all-to-all-start.1 = ((bf16[32,2,768]{2,1,0:T(2,128)(2,1)}), bf16[32,2,768]{2,1,0:T(2,128)(2,1)S(1)}, u32[]{:S(2)}, u32[]{:S(2)}) async-start(bf16[32,2,768]{2,1,0:T(2,128)(2,1)} %reshape.216), calls=%async_computation.1 | async-start | bytes 196608 | tf_op jit(solution)/shard_map/all_to_all | solution.py:52
  23.5 173.5 %all-gather.9.cloned.1.call-start = ((), (), s32[]{:S(2)}) async-start(), calls=%async_computation.12 | async-start | bytes 4866048 | tf_op jit(solution)/shard_map/all_gather | solution.py:165
  25.2 53.1 %copy-start.12 = (bf16[256,768]{1,0:T(8,128)(2,1)S(1)}, bf16[256,768]{1,0:T(8,128)(2,1)}, u32[]{:S(2)}) copy-start(bf16[256,768]{1,0:T(8,128)(2,1)} %param.16) | copy-start | bytes 1179652
  41.5 19.1 %all-to-all-start = ((bf16[8,16,768]{2,1,0:T(8,128)(2,1)}), bf16[8,16,768]{2,1,0:T(8,128)(2,1)S(1)}, u32[]{:S(2)}, u32[]{:S(2)}) async-start(bf16[8,16,768]{2,1,0:T(8,128)(2,1)} %broadcast_in_dim.52), calls=%async_computation | async-start | bytes 393216 | tf_op jit(solution)/shard_map/all_to_all | solution.py:43
  61.4 17.6 %all-to-all-start.2 = ((bf16[32,3,768]{2,1,0:T(4,128)(2,1)}), bf16[32,3,768]{2,1,0:T(4,128)(2,1)S(1)}, u32[]{:S(2)}, u32[]{:S(2)}) async-start(bf16[32,3,768]{2,1,0:T(4,128)(2,1)} %broadcast_in_dim.53), calls=%async_computation.2 | async-start | bytes 393216 | tf_op jit(solution)/shard_map/all_to_all | solution.py:43
  79.0 1.9 copy-start.8
  80.9 12.8 %all-to-all-start.3 = ((bf16[32,2,768]{2,1,0:T(2,128)(2,1)}), bf16[32,2,768]{2,1,0:T(2,128)(2,1)S(1)}, u32[]{:S(2)}, u32[]{:S(2)}) async-start(bf16[32,2,768]{2,1,0:T(2,128)(2,1)} %reshape.240), calls=%async_computation.3 | async-start | bytes 196608 | tf_op jit(solution)/shard_map/all_to_all | solution.py:43
  93.9 29.6 %copy-start.2 = (f32[64,768]{1,0:T(8,128)S(1)}, f32[64,768]{1,0:T(8,128)}, u32[]{:S(2)}) copy-start(f32[64,768]{1,0:T(8,128)} %param.22) | copy-start | bytes 589828
  95.6 15.8 %all-to-all-start.4 = ((bf16[32,3,768]{2,1,0:T(4,128)(2,1)}), bf16[32,3,768]{2,1,0:T(4,128)(2,1)S(1)}, u32[]{:S(2)}, u32[]{:S(2)}) async-start(bf16[32,3,768]{2,1,0:T(4,128)(2,1)} %pad_maximum_fusion.2), calls=%async_computation.4 | async-start | bytes 393216 | tf_op jit(solution)/shard_map/all_to_all | solution.py:52
  112.5 10.9 %all-to-all-start.5 = ((bf16[32,2,768]{2,1,0:T(2,128)(2,1)}), bf16[32,2,768]{2,1,0:T(2,128)(2,1)S(1)}, u32[]{:S(2)}, u32[]{:S(2)}) async-start(bf16[32,2,768]{2,1,0:T(2,128)(2,1)} %broadcast_in_dim.59), calls=%async_computation.5 | async-start | bytes 196608 | tf_op jit(solution)/shard_map/all_to_all | solution.py:43
  134.8 3.9 %copy-start.4 = (bf16[256,768]{1,0:T(8,128)(2,1)}, bf16[256,768]{1,0:T(8,128)(2,1)S(1)}, u32[]{:S(2)}) copy-start(bf16[256,768]{1,0:T(8,128)(2,1)S(1)} %convolution_convert_fusion.1) | copy-start | bytes 1179652
  136.1 13.4 %all-to-all-start.6 = ((bf16[32,3,768]{2,1,0:T(4,128)(2,1)}), bf16[32,3,768]{2,1,0:T(4,128)(2,1)S(1)}, u32[]{:S(2)}, u32[]{:S(2)}) async-start(bf16[32,3,768]{2,1,0:T(4,128)(2,1)} %pad_maximum_fusion.3), calls=%async_computation.6 | async-start | bytes 393216 | tf_op jit(solution)/shard_map/all_to_all | solution.py:52
  150.6 11.0 %all-to-all-start.7 = ((bf16[32,2,768]{2,1,0:T(2,128)(2,1)}), bf16[32,2,768]{2,1,0:T(2,128)(2,1)S(1)}, u32[]{:S(2)}, u32[]{:S(2)}) async-start(bf16[32,2,768]{2,1,0:T(2,128)(2,1)} %broadcast_in_dim.63), calls=%async_computation.7 | async-start | bytes 196608 | tf_op jit(solution)/shard_map/all_to_all | solution.py:43
  161.6 2.8 %copy-start.3 = (f32[64,2304]{1,0:T(8,128)S(1)}, f32[64,2304]{1,0:T(8,128)}, u32[]{:S(2)}) copy-start(f32[64,2304]{1,0:T(8,128)} %fusion.2) | copy-start | bytes 1769476
  164.5 1.0 copy-start.5
  166.8 15.1 %all-to-all-start.8 = ((bf16[32,3,768]{2,1,0:T(4,128)(2,1)}), bf16[32,3,768]{2,1,0:T(4,128)(2,1)S(1)}, u32[]{:S(2)}, u32[]{:S(2)}) async-start(bf16[32,3,768]{2,1,0:T(4,128)(2,1)} %pad_maximum_fusion.4), calls=%async_computation.8 | async-start | bytes 393216 | tf_op jit(solution)/shard_map/all_to_all | solution.py:52
  169.6 2.7 %copy-start.9 = (bf16[32,3,768]{2,1,0:T(4,128)(2,1)S(1)}, bf16[32,3,768]{2,1,0:T(4,128)(2,1)}, u32[]{:S(2)}) copy-start(bf16[32,3,768]{2,1,0:T(4,128)(2,1)} %copy-done.8) | copy-start | bytes 442372
  183.0 11.0 %all-to-all-start.9 = ((bf16[32,2,768]{2,1,0:T(2,128)(2,1)}), bf16[32,2,768]{2,1,0:T(2,128)(2,1)S(1)}, u32[]{:S(2)}, u32[]{:S(2)}) async-start(bf16[32,2,768]{2,1,0:T(2,128)(2,1)} %broadcast_in_dim.67), calls=%async_computation.9 | async-start | bytes 196608 | tf_op jit(solution)/shard_map/all_to_all | solution.py:43
  196.9 5.2 %copy-start.7 = (f32[64,768]{1,0:T(8,128)}, f32[64,768]{1,0:T(8,128)S(1)}, u32[]{:S(2)}) copy-start(f32[64,768]{1,0:T(8,128)S(1)} %fusion.51) | copy-start | bytes 589828
  199.4 2.8 %copy-start.1 = (f32[1024,768]{1,0:T(8,128)S(1)}, f32[1024,768]{1,0:T(8,128)}, u32[]{:S(2)}) copy-start(f32[1024,768]{1,0:T(8,128)} %fusion.12) | copy-start | bytes 9437188
  202.9 2.7 %copy-start.6 = (bf16[1024,768]{1,0:T(8,128)(2,1)}, bf16[1024,768]{1,0:T(8,128)(2,1)S(1)}, u32[]{:S(2)}) copy-start(bf16[1024,768]{1,0:T(8,128)(2,1)S(1)} %add_convert_fusion) | copy-start | bytes 4718596
  216.3 21.2 %all-to-all-start.10 = ((bf16[8,100,384]{2,1,0:T(8,128)(2,1)}), bf16[8,100,384]{2,1,0:T(8,128)(2,1)S(1)}, u32[]{:S(2)}, u32[]{:S(2)}) async-start(bf16[8,100,384]{2,1,0:T(8,128)(2,1)} %pad_maximum_fusion.1), calls=%async_computation.10 | async-start | bytes 1277952 | tf_op jit(solution)/shard_map/all_to_all | solution.py:52
Sparse Core Ops, SparseCore 0:
  12.4 101.8 all-gather.6
  117.1 66.9 all-gather.8

commit v2 on v1

v2 whole, which is shorter than its diff:
```python
import jax
import jax.numpy as jnp
from jax import lax
from jax.experimental import pallas as pl
from jax.experimental.pallas import tpu as pltpu
from jax.sharding import PartitionSpec as P

ITERS = 3


EPSILON = 1e-05
ATTN_FLOOR = 1e-08
BOTH = ("tok", "rep")
F32 = jnp.float32
BF16 = jnp.bfloat16
LANES = 128


def normalize(values):
    mean = jnp.mean(values, axis=-1, keepdims=True)
    centred = values - mean
    spread = jnp.mean(centred * centred, axis=-1, keepdims=True)
    return centred * lax.rsqrt(spread + EPSILON)


def dot(left, right, left_dim=1, right_dim=0):
    return lax.dot_general(
        left, right, (((left_dim,), (right_dim,)), ((), ())), preferred_element_type=F32
    )


def lookup(table, index):
    onehot = (index[:, None] == jnp.arange(table.shape[0], dtype=jnp.int32)[None, :]).astype(BF16)
    return dot(onehot, table)


def spread_out(chunk, axis):
    copies = lax.axis_size(axis)
    return lax.all_to_all(jnp.broadcast_to(chunk[None], (copies,) + chunk.shape), axis, 0, 0)


def sum_chunks(pieces, axis):
    return jnp.sum(lax.all_to_all(pieces.astype(BF16), axis, 0, 0).astype(F32), axis=0)


def widen(block, axis, mask, spot):
    ring = [(i, i ^ mask) for i in range(lax.axis_size(axis))]
    upper = (lax.axis_index(axis) // mask) % 2 == 1
    got = lax.ppermute(block, axis, ring)
    return jnp.stack([jnp.where(upper, got, block), jnp.where(upper, block, got)], axis=spot)


def stages(axes):
    spots = []
    for axis in axes:
        mask = lax.axis_size(axis) // 2
        while mask:
            spots.append((axis, mask))
            mask //= 2
    return spots


def double(block, axis, spot=0):
    for extra, (over, mask) in enumerate(stages((axis,))):
        block = widen(block, over, mask, spot + extra)
    return block


def after(value, *earlier):
    return lax.optimization_barrier((value,) + earlier)[0]


def pack(weights):
    reps = lax.axis_size("rep")
    size = weights[0].shape[0] // reps
    widths = [weight.shape[1] for weight in weights]
    if size % 8:
        start = lax.axis_index("rep") * size
        return jnp.concatenate(
            [lax.dynamic_slice_in_dim(weight, start, size, 0) for weight in weights], axis=1
        )

    def body(rep_ref, *refs):
        column = 0
        for source, wide in zip(refs[:-1], widths):
            refs[-1][:, column : column + wide] = source[...]
            column += wide

    return pl.pallas_call(
        body,
        grid_spec=pltpu.PrefetchScalarGridSpec(
            num_scalar_prefetch=1,
            grid=(1,),
            in_specs=[pl.BlockSpec((size, wide), lambda i, rep: (rep[0], 0)) for wide in widths],
            out_specs=pl.BlockSpec((size, sum(widths)), lambda i, rep: (0, 0)),
        ),
        out_shape=jax.ShapeDtypeStruct((size, sum(widths)), weights[0].dtype),
        name="pack",
    )(lax.axis_index("rep").reshape(1), *weights)


def gru(slots, update, gru_input, gru_hidden):
    width = slots.shape[1]
    from_update = dot(update, gru_input)
    from_state = dot(slots.astype(BF16), gru_hidden)
    reset = jax.nn.sigmoid(from_update[:, :width] + from_state[:, :width])
    blend = jax.nn.sigmoid(from_update[:, width : 2 * width] + from_state[:, width : 2 * width])
    candidate = jnp.tanh(from_update[:, 2 * width :] + reset * from_state[:, 2 * width :])
    return (1.0 - blend) * candidate + blend * slots


def on_device(
    patches,
    patch_view,
    rays,
    ray_view,
    targets,
    camera,
    slots_init,
    key_weight,
    value_weight,
    query_weight,
    gru_input,
    gru_hidden,
    mix_query,
    mix_key,
    render_in,
    render_out,
):
    width = patches.shape[1]
    scale = width ** (-0.5)
    slot_count = slots_init.shape[0]
    toks, reps = lax.axis_size("tok"), lax.axis_size("rep")
    parts = toks * reps
    rep = lax.axis_index("rep")

    def piece(rows):
        size = rows.shape[0] // reps
        return lax.dynamic_slice_in_dim(rows, rep * size, size, 0)

    first = pack([key_weight, value_weight, query_weight, gru_input, gru_hidden])
    first = lax.all_gather(first, BOTH, axis=0, tiled=True)

    table = double(spread_out(piece(camera), "tok"), "rep", 1).reshape(-1, width)

    colours = render_out.shape[0]
    of_rep = slot_count // reps
    depth = query_weight.shape[0]
    start = lax.dynamic_slice_in_dim(normalize(slots_init).astype(BF16), rep * of_rep, of_rep, 0)
    start = lax.dynamic_slice_in_dim(start, lax.axis_index("tok") * depth, depth, 1)
    flat = render_out.reshape(-1)
    extra_rows = -(-flat.shape[0] // width)
    flat = jnp.pad(flat, (0, extra_rows * width - flat.shape[0])).reshape(extra_rows, width)
    got = spread_out(jnp.concatenate([dot(start, query_weight).astype(BF16), flat], axis=0), "tok")
    query = (jnp.sum(got[:, :of_rep].astype(F32), axis=0) * scale).astype(BF16)
    colour_full = got[:, of_rep:].reshape(toks, -1)[:, : render_out.size]
    colour_full = colour_full.reshape(toks, colours, -1).transpose(1, 0, 2).reshape(colours, -1)
    reach = spread_out(dot(query, key_weight, 1, 1).astype(BF16), BOTH)
    reach = reach.reshape(toks, reps, of_rep, depth).transpose(1, 2, 0, 3).reshape(slot_count, width)

    whole_rows = slot_count % parts == 0
    patch_x = normalize(patches.astype(F32) + lookup(table, patch_view)).astype(BF16)
    ones = jnp.ones((patches.shape[0], LANES), BF16)

    def gather_update(logits, source):
        attn = jax.nn.softmax(logits, axis=1) + ATTN_FLOOR
        numer = dot(attn.astype(BF16), source, 0, 0)
        if whole_rows:
            total = sum_chunks(numer.reshape(parts, -1, numer.shape[1]), BOTH)
            part = (total[:, :width] / total[:, width : width + 1]).astype(BF16)
            return spread_out(part, BOTH).reshape(slot_count, width)
        total = spread_out(sum_chunks(numer.reshape(parts, -1), BOTH), BOTH).reshape(numer.shape)
        return (total[:, :width] / total[:, width : width + 1]).astype(BF16)

    seen = gather_update(dot(patch_x, reach, 1, 1), jnp.concatenate([patch_x, ones], axis=1))

    keys = dot(patch_x, first[:, :width]).astype(BF16)
    value_full = first[:, width : 2 * width]
    values = jnp.concatenate([dot(patch_x, value_full).astype(BF16), ones], axis=1)
    reached = (dot(keys, first[:, 2 * width : 3 * width], 1, 1) * scale).astype(BF16)
    input_full, hidden_full = first[:, 3 * width : 6 * width], first[:, 6 * width :]

    mixer_full = lax.all_gather(
        after(pack([mix_query, mix_key]), first), BOTH, axis=0, tiled=True
    )
    units = render_in.shape[1] // reps
    head = lax.dynamic_slice_in_dim(render_in, rep * units, units, 1)
    mixer = (dot(mixer_full[:, :width], mixer_full[:, width:], 1, 1) * scale).astype(BF16)

    slots = gru(slots_init, dot(seen, value_full).astype(BF16), input_full, hidden_full)
    ray_rows = rays.shape[0]
    aside = jnp.concatenate([targets, ray_view.astype(F32)[None]], axis=0)
    group, aside, head = after(rays, slots), after(aside, slots), after(head, slots)
    waiting = [stages(("rep",)), stages(("tok",))]
    spot = 0
    for step in range(1, ITERS):
        logits = dot(reached, normalize(slots).astype(BF16), 1, 1)
        last = step == ITERS - 1
        while spot < step or (last and spot < max(map(len, waiting))):
            for over, mask in waiting[0][spot : spot + 1]:
                group, aside = widen(group, over, mask, spot), widen(aside, over, mask, spot)
            for over, mask in waiting[1][spot : spot + 1]:
                head = widen(head, over, mask, spot)
            spot += 1
        seen = gather_update(logits, values)
        if last:
            seen = after(seen, mixer)
        else:
            group, aside, head = after(group, seen), after(aside, seen), after(head, seen)
        slots = gru(slots, seen, input_full, hidden_full)
    head = head.reshape(width, units)
    group = group.reshape(reps * ray_rows, width)
    aside = aside.reshape(reps, colours + 1, ray_rows)
    aside = aside.transpose(1, 0, 2).reshape(colours + 1, -1)
    group_targets, group_view = aside[:colours], aside[colours].astype(jnp.int32)
    ray_in = group.astype(F32) + lookup(table, group_view)
    ray_x = ray_in.astype(BF16)

    slots_low = slots.astype(BF16)
    mixer = dot(mixer, slots_low, 1, 1).astype(BF16)
    mix = jax.nn.softmax(dot(ray_x, mixer), axis=1).astype(BF16)
    joined = (dot(mix, slots_low) + ray_in).astype(BF16)

    colour_head = lax.dynamic_slice_in_dim(colour_full, rep * units, units, 1)
    pre = dot(joined, head)
    sig = jax.nn.sigmoid(pre)
    hidden = (pre * sig).astype(BF16)
    colour = jnp.sum(lax.all_gather(dot(colour_head, hidden, 1, 1), "rep", axis=0), axis=0)
    error = colour - group_targets
    rays_total = ray_rows * parts
    dcol = (error * (2.0 / jnp.sqrt(jnp.float32(3.0 * rays_total)))).astype(BF16)
    squared = jnp.sum(error * error)
    out_part = dot(dcol, hidden)
    dhidden = dot(dcol, colour_head, 0, 0)
    dpre = (dhidden * (sig + pre * sig * (1.0 - sig))).astype(BF16)
    grad = dot(joined, dpre, 0, 0)
    below = jnp.concatenate([out_part, jnp.broadcast_to(squared, (1, units))], axis=0).astype(BF16)
    mine = width // toks
    below = jnp.broadcast_to(below[None], (toks,) + below.shape)
    grad = jnp.concatenate([grad.astype(BF16).reshape(toks, mine, units), below], axis=1)
    total = lax.all_gather(sum_chunks(grad, "tok"), "rep", axis=1, tiled=True)
    return (
        slots,
        lax.dynamic_slice_in_dim(colour, rep * ray_rows, ray_rows, 1),
        total[mine + colours, 0] / (3.0 * rays_total),
        total[:mine],
        total[mine : mine + colours],
    )


def solution(mesh):
    placed = (
        P(("tok", "rep"), None),
        P(("tok", "rep")),
        P(("tok", "rep"), None),
        P(("tok", "rep")),
        P(None, ("tok", "rep")),
        P("tok", None),
        P(),
        P("tok", None),
        P("tok", None),
        P("tok", None),
        P("tok", None),
        P("tok", None),
        P("tok", None),
        P("tok", None),
        P("tok", None),
        P(None, "tok"),
    )
    return jax.shard_map(
        on_device,
        mesh=mesh,
        in_specs=placed,
        out_specs=(P(), P(None, ("tok", "rep")), P(), P("tok", None), P()),
        check_vma=False,
    )
```

time: 257 us -> 245 us (0.953)
  blocking collectives: 50.2 us -> 12.4 us
  waiting for transfers between devices: 76.5 us -> 103 us
  other arithmetic: 12 us -> 8.15 us
  starting transfers between devices: 42.9 us -> 46.4 us
  Pallas kernels: 0 us -> 3.28 us
    all_gather x5 -> x1, blocking collectives: 45 us -> 7.04 us  [on_device(): total = lax.all_gather(sum_chunks(grad, 'tok'), 'rep', axis=1, tiled=True)]
    all_gather x1, waiting for transfers between devices: 0.02 us -> 21.8 us  [on_device(): first = lax.all_gather(first, BOTH, axis=0, tiled=True)]
    all_to_all x6, waiting for transfers between devices: 38 us -> 50.6 us  [spread_out(): lax.all_to_all(jnp.broadcast_to(chunk[None], (copies,) + chunk.shape), ax...]
    all_to_all x5 -> x4, waiting for transfers between devices: 38.4 us -> 27.5 us  [sum_chunks(): lax.all_to_all(pieces.astype(BF16), axis, 0, 0).astype(F32)]
    ppermute x0 -> x9, starting transfers between devices: none -> 10.2 us  [widen(): got = lax.ppermute(block, axis, ring)]
    all_to_all x5 -> x4, starting transfers between devices: 18.8 us -> 12.8 us  [sum_chunks(): lax.all_to_all(pieces.astype(BF16), axis, 0, 0).astype(F32)]
    concatenate x7 -> x2, other arithmetic: 5.72 us -> 0.9 us  [the longest x1 0.89 us: on_device(): jnp.concatenate([grad.astype(BF16).reshape(toks, mine, units), below], ax...]
    unnamed x40 -> x41, local copies, waits for them, and re-layouts: 5.35 us -> 1.71 us
  transfers between devices with their start and end apart: 13 -> 21, of which waited for: 9 -> 12; matrix products, arithmetic and copies ran while one was open for 19% -> 15% of each run, Pallas kernels for 0% -> 1%
where the time goes in v2:
time: 245 us; the launch traced here: 244 us
  waiting for transfers between devices  103 us (42%)
  starting transfers between devices  46.4 us (19%)
  matrix products  39.6 us (16%)
  between operations  16.6 us (7%)
  local copies, waits for them, and re-layouts  14.1 us (6%)
  blocking collectives  12.4 us (5%)
  other arithmetic  8.15 us (3%)
  Pallas kernels  3.28 us (1%)
    all_to_all x6, waiting for transfers between devices, spread_out(): lax.all_to_all(jnp.broadcast_to(chunk[None], (copies,) + chunk.shape), ax...  50.6 us
    dot_general x25, matrix products, dot(): lax.dot_general(left, right, (((left_dim,), (right_dim,)), ((), ())), pre...  39.6 us
    all_to_all x4, waiting for transfers between devices, sum_chunks(): lax.all_to_all(pieces.astype(BF16), axis, 0, 0).astype(F32)  27.5 us
    all_to_all x6, starting transfers between devices, spread_out(): lax.all_to_all(jnp.broadcast_to(chunk[None], (copies,) + chunk.shape), ax...  23.4 us
    all_gather x1, waiting for transfers between devices, on_device(): first = lax.all_gather(first, BOTH, axis=0, tiled=True)  21.8 us
    all_to_all x4, starting transfers between devices, sum_chunks(): lax.all_to_all(pieces.astype(BF16), axis, 0, 0).astype(F32)  12.8 us
    ppermute x9, starting transfers between devices, widen(): got = lax.ppermute(block, axis, ring)  10.2 us
    all_gather x1, blocking collectives, on_device(): total = lax.all_gather(sum_chunks(grad, 'tok'), 'rep', axis=1, tiled=True)  7.04 us
  transfers between devices with their start and end apart: 21, of which 12 were waited for; matrix products, arithmetic and copies ran while one was open for 15% of the time, Pallas kernels for 1%

profile of v2, /device:TPU:0, one launch (start us, length us, event | category | flops | bytes accessed | tf_op | source)
XLA Modules:
  0.0 243.9 jit_solution(8337895396295399512)
XLA Ops:
  7.3 1.9 pack.2
  9.1 0.7 constant_dynamic-slice_fusion.2
  9.9 0.7 broadcast_in_dim.16
  10.6 7.3 %all-to-all-start = ((bf16[8,16,768]{2,1,0:T(8,128)(2,1)}), bf16[8,16,768]{2,1,0:T(8,128)(2,1)S(1)}, u32[]{:S(2)}, u32[]{:S(2)}) async-start(bf16[8,16,768]{2,1,0:T(8,128)(2,1)} %broadcast_in_dim.16), calls=%async_computation | async-start | bytes 393216 | tf_op jit(solution)/shard_map/all_to_all | solution.py:39
  18.7 7.3 %all-to-all-done = bf16[8,16,768]{2,1,0:T(8,128)(2,1)S(1)} async-done(((bf16[8,16,768]{2,1,0:T(8,128)(2,1)}), bf16[8,16,768]{2,1,0:T(8,128)(2,1)S(1)}, u32[]{:S(2)}, u32[]{:S(2)}) %all-to-all-start) | async-done | bytes 196640 | tf_op jit(solution)/shard_map/all_to_all | solution.py:39
  25.9 0.7 broadcast_in_dim.17
  26.7 3.4 %all-to-all-start.1 = ((bf16[8,17,768]{2,1,0:T(8,128)(2,1)}), bf16[8,17,768]{2,1,0:T(8,128)(2,1)S(1)}, u32[]{:S(2)}, u32[]{:S(2)}) async-start(bf16[8,17,768]{2,1,0:T(8,128)(2,1)} %broadcast_in_dim.17), calls=%async_computation.1 | async-start | bytes 589824 | tf_op jit(solution)/shard_map/all_to_all | solution.py:39
  30.1 1.6 collective-permute-start
  31.7 10.0 %all-to-all-done.1 = bf16[8,17,768]{2,1,0:T(8,128)(2,1)S(1)} async-done(((bf16[8,17,768]{2,1,0:T(8,128)(2,1)}), bf16[8,17,768]{2,1,0:T(8,128)(2,1)S(1)}, u32[]{:S(2)}, u32[]{:S(2)}) %all-to-all-start.1) | async-done | bytes 208928 | tf_op jit(solution)/shard_map/all_to_all | solution.py:39
  42.0 0.7 broadcast_in_dim.18
  42.7 3.7 %all-to-all-start.2 = ((bf16[32,16,96]{2,1,0:T(8,128)(2,1)}), bf16[32,16,96]{2,1,0:T(8,128)(2,1)S(1)}, u32[]{:S(2)}, u32[]{:S(2)}) async-start(bf16[32,16,96]{2,1,0:T(8,128)(2,1)} %broadcast_in_dim.18), calls=%async_computation.2 | async-start | bytes 262144 | tf_op jit(solution)/shard_map/all_to_all | solution.py:39
  46.5 10.7 %all-to-all-done.2 = bf16[32,16,96]{2,1,0:T(8,128)(2,1)S(1)} async-done(((bf16[32,16,96]{2,1,0:T(8,128)(2,1)}), bf16[32,16,96]{2,1,0:T(8,128)(2,1)S(1)}, u32[]{:S(2)}, u32[]{:S(2)}) %all-to-all-start.2) | async-done | bytes 98336 | tf_op jit(solution)/shard_map/all_to_all | solution.py:39
  57.6 0.8 copy-done.12
  59.8 0.7 convert_element_type.161
  60.5 3.5 %all-to-all-start.3 = ((bf16[32,2,896]{2,1,0:T(2,128)(2,1)}), bf16[32,2,896]{2,1,0:T(2,128)(2,1)S(1)}, u32[]{:S(2)}, u32[]{:S(2)}) async-start(bf16[32,2,896]{2,1,0:T(2,128)(2,1)} %convert_element_type.161), calls=%async_computation.3 | async-start | bytes 229376 | tf_op jit(solution)/shard_map/all_to_all | solution.py:43
  64.1 1.4 pack.3
  65.5 6.5 %all-to-all-done.3 = bf16[32,2,896]{2,1,0:T(2,128)(2,1)S(1)} async-done(((bf16[32,2,896]{2,1,0:T(2,128)(2,1)}), bf16[32,2,896]{2,1,0:T(2,128)(2,1)S(1)}, u32[]{:S(2)}, u32[]{:S(2)}) %all-to-all-start.3) | async-done | bytes 114720 | tf_op jit(solution)/shard_map/all_to_all | solution.py:43
  72.3 0.7 broadcast_in_dim.19
  73.0 2.6 %all-to-all-start.4 = ((bf16[32,2,768]{2,1,0:T(2,128)(2,1)}), bf16[32,2,768]{2,1,0:T(2,128)(2,1)S(1)}, u32[]{:S(2)}, u32[]{:S(2)}) async-start(bf16[32,2,768]{2,1,0:T(2,128)(2,1)} %broadcast_in_dim.19), calls=%async_computation.4 | async-start | bytes 196608 | tf_op jit(solution)/shard_map/all_to_all | solution.py:39
  75.9 0.7 reshape.153
  76.6 8.5 %all-to-all-done.4 = bf16[32,2,768]{2,1,0:T(2,128)(2,1)S(1)} async-done(((bf16[32,2,768]{2,1,0:T(2,128)(2,1)}), bf16[32,2,768]{2,1,0:T(2,128)(2,1)S(1)}, u32[]{:S(2)}, u32[]{:S(2)}) %all-to-all-start.4) | async-done | bytes 98336 | tf_op jit(solution)/shard_map/all_to_all | solution.py:39
  85.1 21.8 %all-gather.5.cloned.1.call-done = bf16[768,6912]{1,0:T(8,128)(2,1)} async-done(((bf16[24,6912]{1,0:T(8,128)(2,1)}), bf16[768,6912]{1,0:T(8,128)(2,1)}) %all-gather.5.cloned.1.call-update) | async-done | bytes 10616848 | tf_op jit(solution)/shard_map/all_gather | solution.py:142
  106.9 2.7 %convolution_bitcast_fusion = f32[64,2304]{1,0:T(8,128)S(1)} fusion(bf16[768,6912]{1,0:T(8,128)(2,1)} %all-gather.5.cloned.1.call-done, f32[64,768]{1,0:T(8,128)S(1)} %copy-done.5), kind=kOutput, calls=%fused_computation | convolution fusion | flops 226541568 | bytes 4325376 | tf_op jit(solution)/shard_map/dot_general | solution.py:27
  109.6 3.4 %fusion.9 = f32[64,2304]{1,0:T(8,128)S(1)} fusion(bf16[768,6912]{1,0:T(8,128)(2,1)} %all-gather.5.cloned.1.call-done, bf16[64,768]{1,0:T(8,128)(2,1)S(1)} %reshape.148), kind=kOutput, calls=%fused_computation.12 | convolution fusion | flops 302039040 | bytes 5406720 | tf_op jit(solution)/shard_map/dot_general | solution.py:27
  113.5 1.5 collective-permute-start.4
  114.9 2.6 %fusion.14 = bf16[256,768]{1,0:T(8,128)(2,1)S(1)} fusion(bf16[256,768]{1,0:T(8,128)(2,1)S(1)} %multiply_convert_fusion.2, bf16[768,6912]{1,0:T(8,128)(2,1)} %all-gather.5.cloned.1.call-done), kind=kOutput, calls=%fused_computation.26 | convolution fusion | flops 604569600 | bytes 3145728 | tf_op jit(solution)/shard_map/dot_general | solution.py:27
  117.8 1.8 convolution_convert_fusion.1
  119.9 0.7 convert_element_type.170
  120.6 3.2 %all-to-all-start.5 = ((bf16[32,2,896]{2,1,0:T(2,128)(2,1)}), bf16[32,2,896]{2,1,0:T(2,128)(2,1)S(1)}, u32[]{:S(2)}, u32[]{:S(2)}) async-start(bf16[32,2,896]{2,1,0:T(2,128)(2,1)} %convert_element_type.170), calls=%async_computation.5 | async-start | bytes 229376 | tf_op jit(solution)/shard_map/all_to_all | solution.py:43
  123.8 2.7 %collective-permute-start.6 = (bf16[96,384]{1,0:T(8,128)(2,1)S(1)}, bf16[96,384]{1,0:T(8,128)(2,1)S(1)}, u32[]{:S(2)}, u32[]{:S(2)}) collective-permute-start(bf16[96,384]{1,0:T(8,128)(2,1)S(1)} %constant_dynamic-slice_fusion.1), channel_id=1, source_target_pairs={{0,16},{4,20},{8,24},{12,28},{16,0},{20,4},{24,8},{28,12},{1,17},{... | collective-permute-start | bytes 221192 | tf_op jit(solution)/shard_map/ppermute | solution.py:49
  126.5 1.5 collective-permute-start.2
  128.0 2.7 %fusion.2 = f32[64,2304]{1,0:T(8,128)S(1)} fusion(bf16[768,6912]{1,0:T(8,128)(2,1)} %all-gather.5.cloned.1.call-done, f32[64,768]{1,0:T(8,128)S(1)} %get-tuple-element.24), kind=kOutput, calls=%fused_computation.5 | convolution fusion | flops 226541568 | bytes 4325376 | tf_op jit(solution)/shard_map/dot_general | solution.py:27
  130.7 2.6 %collective-permute-done.6 = bf16[96,384]{1,0:T(8,128)(2,1)S(1)} collective-permute-done((bf16[96,384]{1,0:T(8,128)(2,1)S(1)}, bf16[96,384]{1,0:T(8,128)(2,1)S(1)}, u32[]{:S(2)}, u32[]{:S(2)}) %collective-permute-start.6) | collective-permute-done | bytes 73760 | tf_op jit(solution)/shard_map/ppermute | solution.py:49
  133.8 0.7 broadcast_in_dim.20
  134.5 3.6 %all-to-all-start.6 = ((bf16[32,2,768]{2,1,0:T(2,128)(2,1)}), bf16[32,2,768]{2,1,0:T(2,128)(2,1)S(1)}, u32[]{:S(2)}, u32[]{:S(2)}) async-start(bf16[32,2,768]{2,1,0:T(2,128)(2,1)} %broadcast_in_dim.20), calls=%async_computation.6 | async-start | bytes 196608 | tf_op jit(solution)/shard_map/all_to_all | solution.py:39
  138.1 0.8 collective-permute-done.2
  139.0 7.3 %all-to-all-done.6 = bf16[32,2,768]{2,1,0:T(2,128)(2,1)S(1)} async-done(((bf16[32,2,768]{2,1,0:T(2,128)(2,1)}), bf16[32,2,768]{2,1,0:T(2,128)(2,1)S(1)}, u32[]{:S(2)}, u32[]{:S(2)}) %all-to-all-start.6) | async-done | bytes 98336 | tf_op jit(solution)/shard_map/all_to_all | solution.py:39
  147.3 2.7 %fusion.7 = f32[64,2304]{1,0:T(8,128)S(1)} fusion(bf16[64,768]{1,0:T(8,128)(2,1)S(1)} %reshape.149, bf16[768,6912]{1,0:T(8,128)(2,1)} %all-gather.5.cloned.1.call-done), kind=kOutput, calls=%fused_computation.10 | convolution fusion | flops 226492416 | bytes 4227072 | tf_op jit(solution)/shard_map/dot_general | solution.py:27
  151.1 0.7 convert_element_type.177
  151.8 2.5 %all-to-all-start.7 = ((bf16[32,2,896]{2,1,0:T(2,128)(2,1)}), bf16[32,2,896]{2,1,0:T(2,128)(2,1)S(1)}, u32[]{:S(2)}, u32[]{:S(2)}) async-start(bf16[32,2,896]{2,1,0:T(2,128)(2,1)} %convert_element_type.177), calls=%async_computation.7 | async-start | bytes 229376 | tf_op jit(solution)/shard_map/all_to_all | solution.py:43
  154.5 3.6 %fusion = f32[64,2304]{1,0:T(8,128)} fusion(bf16[768,6912]{1,0:T(8,128)(2,1)} %all-gather.5.cloned.1.call-done, f32[64,768]{1,0:T(8,128)S(1)} %get-tuple-element.22), kind=kOutput, calls=%fused_computation.3 | convolution fusion | flops 226541568 | bytes 4325376 | tf_op jit(solution)/shard_map/dot_general | solution.py:27
  158.2 1.7 collective-permute-start.8
  159.9 3.9 %all-to-all-done.7 = bf16[32,2,896]{2,1,0:T(2,128)(2,1)S(1)} async-done(((bf16[32,2,896]{2,1,0:T(2,128)(2,1)}), bf16[32,2,896]{2,1,0:T(2,128)(2,1)S(1)}, u32[]{:S(2)}, u32[]{:S(2)}) %all-to-all-start.7) | async-done | bytes 114720 | tf_op jit(solution)/shard_map/all_to_all | solution.py:43
  164.1 0.7 broadcast_in_dim.21
  164.8 2.7 %all-to-all-start.8 = ((bf16[32,2,768]{2,1,0:T(2,128)(2,1)}), bf16[32,2,768]{2,1,0:T(2,128)(2,1)S(1)}, u32[]{:S(2)}, u32[]{:S(2)}) async-start(bf16[32,2,768]{2,1,0:T(2,128)(2,1)} %broadcast_in_dim.21), calls=%async_computation.8 | async-start | bytes 196608 | tf_op jit(solution)/shard_map/all_to_all | solution.py:39
  168.2 7.0 %all-to-all-done.8 = bf16[32,2,768]{2,1,0:T(2,128)(2,1)S(1)} async-done(((bf16[32,2,768]{2,1,0:T(2,128)(2,1)}), bf16[32,2,768]{2,1,0:T(2,128)(2,1)S(1)}, u32[]{:S(2)}, u32[]{:S(2)}) %all-to-all-start.8) | async-done | bytes 98336 | tf_op jit(solution)/shard_map/all_to_all | solution.py:39
  175.3 0.9 pad_maximum_fusion.3
  176.8 0.8 copy-done.2
  177.6 1.1 bitcast_add_fusion
  178.8 3.8 %multiply_convert_fusion = bf16[768,768]{1,0:T(8,128)(2,1)} fusion(bf16[768,1536]{1,0:T(8,128)(2,1)} %all-gather.7.cloned.1.call-done), kind=kOutput, calls=%fused_computation.14 | convolution fusion | flops 907149312 | bytes 3538944 | tf_op jit(solution)/shard_map/dot_general | solution.py:27
  182.6 2.8 %fusion.5 = f32[64,2304]{1,0:T(8,128)S(1)} fusion(bf16[64,768]{1,0:T(8,128)(2,1)S(1)} %reshape.150, bf16[768,6912]{1,0:T(8,128)(2,1)} %all-gather.5.cloned.1.call-done), kind=kOutput, calls=%fused_computation.8 | convolution fusion | flops 226492416 | bytes 4227072 | tf_op jit(solution)/shard_map/dot_general | solution.py:27
  185.4 0.8 fusion.36
  186.2 3.0 %fusion.124 = (f32[1024]{0:T(1024)S(1)}, f32[1024,64]{0,1:T(8,128)}) fusion(bf16[768,768]{1,0:T(8,128)(2,1)} %multiply_convert_fusion, f32[64,768]{1,0:T(8,128)} %fusion.36, f32[1024,768]{1,0:T(8,128)S(1)} %bitcast_add_fusion), kind=kOutput, calls=%fused_computation.220 | convolution fusion | flops 177110016 | bytes 4788224 | tf_op jit(solution)/shard_map/dot_general | solution.py:27
  189.2 1.0 fusion.32
  190.2 1.7 add_convert_fusion
  191.9 2.2 fusion.22
  194.4 5.4 %all-gather.1 = f32[4,3,1024]{2,1,0:T(4,128)S(1)} all-gather(f32[1,3,1024]{2,1,0:T(4,128)S(1)} %convolution_bitcast_fusion.1), channel_id=2, replica_groups=mesh['tok'=8,'rep'=4] {'rep'}, dimensions={0}, use_global_device_ids=true | all-gather | bytes 61440 | tf_op jit(solution)/shard_map/all_gather | solution.py:228
  200.7 2.7 %convolution_convert_fusion = bf16[768,384]{1,0:T(8,128)(2,1)S(1)} fusion(bf16[1024,768]{1,0:T(8,128)(2,1)S(1)} %copy-done.8, bf16[3,1024]{1,0:T(4,128)(2,1)S(1)} %multiply_convert_fusion.9, f32[1024,384]{1,0:T(8,128)} %get-tuple-element.58, bf16[3,1536]{1,0:T(4,128)(2,1)S(1)} %copy-done.14, s32[]{:T(128)S(6)} %select_n.186), kind=kOutput, calls=%fused_computation.22 | convolution fusion | flops 610172928 | bytes 3746820 | tf_op jit(solution)/shard_map/dot_general | solution.py:27
  203.4 0.7 concatenate.22
  204.0 0.9 pad_maximum_fusion.2
  204.9 3.5 %all-to-all-start.9 = ((bf16[8,100,384]{2,1,0:T(8,128)(2,1)}), bf16[8,100,384]{2,1,0:T(8,128)(2,1)S(1)}, u32[]{:S(2)}, u32[]{:S(2)}) async-start(bf16[8,100,384]{2,1,0:T(8,128)(2,1)} %pad_maximum_fusion.2), calls=%async_computation.9 | async-start | bytes 1277952 | tf_op jit(solution)/shard_map/all_to_all | solution.py:43
  209.1 17.1 %all-to-all-done.9 = bf16[8,100,384]{2,1,0:T(8,128)(2,1)S(1)} async-done(((bf16[8,100,384]{2,1,0:T(8,128)(2,1)}), bf16[8,100,384]{2,1,0:T(8,128)(2,1)S(1)}, u32[]{:S(2)}, u32[]{:S(2)}) %all-to-all-start.9) | async-done | bytes 614432 | tf_op jit(solution)/shard_map/all_to_all | solution.py:43
  226.3 7.0 %all_gather.19 = f32[100,1536]{1,0:T(8,128)S(1)} all-gather(f32[100,384]{1,0:T(8,128)S(1)} %convert_reduce_fusion), channel_id=1, replica_groups=mesh['tok'=8,'rep'=4] {'rep'}, dimensions={1}, use_global_device_ids=true | all-gather | bytes 768000 | tf_op jit(solution)/shard_map/all_gather | solution.py:241
  234.4 0.9 slice.198
  (141 shorter events, 11.9 us)
Async XLA Ops:
  7.2 68.5 %copy-start = (bf16[96,1536]{1,0:T(8,128)(2,1)S(1)}, bf16[96,1536]{1,0:T(8,128)(2,1)}, u32[]{:S(2)}) copy-start(bf16[96,1536]{1,0:T(8,128)(2,1)} %param.30) | copy-start | bytes 884740
  7.2 10.7 %copy-start.5 = (f32[64,768]{1,0:T(8,128)S(1)}, f32[64,768]{1,0:T(8,128)}, u32[]{:S(2)}) copy-start(f32[64,768]{1,0:T(8,128)} %param.22) | copy-start | bytes 589828
  7.2 99.6 %all-gather.5.cloned.1.call-start = ((), (), s32[]{:S(2)}) async-start(), calls=%async_computation.10 | async-start | bytes 10948608 | tf_op jit(solution)/shard_map/all_gather | solution.py:142
  7.2 11.0 %copy-start.17 = (bf16[3,192]{1,0:T(4,128)(2,1)S(1)}, bf16[3,192]{1,0:T(4,128)(2,1)}, u32[]{:S(2)}) copy-start(bf16[3,192]{1,0:T(4,128)(2,1)} %param.31) | copy-start | bytes 3460
  7.3 11.2 %copy-start.9 = (bf16[96,768]{1,0:T(8,128)(2,1)S(1)}, bf16[96,768]{1,0:T(8,128)(2,1)}, u32[]{:S(2)}) copy-start(bf16[96,768]{1,0:T(8,128)(2,1)} %refs_2_.1) | copy-start | bytes 442372
  10.6 15.4 %all-to-all-start = ((bf16[8,16,768]{2,1,0:T(8,128)(2,1)}), bf16[8,16,768]{2,1,0:T(8,128)(2,1)S(1)}, u32[]{:S(2)}, u32[]{:S(2)}) async-start(bf16[8,16,768]{2,1,0:T(8,128)(2,1)} %broadcast_in_dim.16), calls=%async_computation | async-start | bytes 393216 | tf_op jit(solution)/shard_map/all_to_all | solution.py:39
  18.2 23.6 %copy-start.10 = (bf16[96,768]{1,0:T(8,128)(2,1)S(1)}, bf16[96,768]{1,0:T(8,128)(2,1)}, u32[]{:S(2)}) copy-start(bf16[96,768]{1,0:T(8,128)(2,1)} %refs_0_.2) | copy-start | bytes 442372
  26.7 15.0 %all-to-all-start.1 = ((bf16[8,17,768]{2,1,0:T(8,128)(2,1)}), bf16[8,17,768]{2,1,0:T(8,128)(2,1)S(1)}, u32[]{:S(2)}, u32[]{:S(2)}) async-start(bf16[8,17,768]{2,1,0:T(8,128)(2,1)} %broadcast_in_dim.17), calls=%async_computation.1 | async-start | bytes 589824 | tf_op jit(solution)/shard_map/all_to_all | solution.py:39
  30.1 11.6 %collective-permute-start = (bf16[8,16,768]{2,1,0:T(8,128)(2,1)S(1)}, bf16[8,16,768]{2,1,0:T(8,128)(2,1)S(1)}, u32[]{:S(2)}, u32[]{:S(2)}) collective-permute-start(bf16[8,16,768]{2,1,0:T(8,128)(2,1)S(1)} %all-to-all-done), channel_id=1, source_target_pairs={{0,2},{1,3},{2,0},{3,1},{4,6},{5,7},{6,4},{7,5},{8,10},{9,11},{10,... | collective-permute-start | bytes 589832 | tf_op jit(solution)/shard_map/ppermute | solution.py:49
  41.8 15.6 %collective-permute-start.1 = (bf16[8,2,16,768]{3,2,1,0:T(8,128)(2,1)S(1)}, bf16[8,2,16,768]{3,2,1,0:T(8,128)(2,1)S(1)}, u32[]{:S(2)}, u32[]{:S(2)}) collective-permute-start(bf16[8,2,16,768]{3,2,1,0:T(8,128)(2,1)S(1)} %pad_maximum_fusion.4), channel_id=1, source_target_pairs={{0,1},{1,0},{2,3},{3,2},{4,5},{5,4},{6,7},{7,6},{8,9},{9,8},{10,11... | collective-permute-start | bytes 1179656 | tf_op jit(solution)/shard_map/ppermute | solution.py:49
  42.7 14.4 %all-to-all-start.2 = ((bf16[32,16,96]{2,1,0:T(8,128)(2,1)}), bf16[32,16,96]{2,1,0:T(8,128)(2,1)S(1)}, u32[]{:S(2)}, u32[]{:S(2)}) async-start(bf16[32,16,96]{2,1,0:T(8,128)(2,1)} %broadcast_in_dim.18), calls=%async_computation.2 | async-start | bytes 262144 | tf_op jit(solution)/shard_map/all_to_all | solution.py:39
  57.4 1.0 copy-start.12
  57.4 1.0 copy-start.18
  57.5 1.7 copy-start.1
  59.1 5.0 %copy-start.19 = (s32[256]{0:T(256)S(1)}, s32[256]{0:T(256)}, u32[]{:S(2)}) copy-start(s32[256]{0:T(256)} %param.19) | copy-start | bytes 3076
  59.3 16.4 %copy-start.16 = (f32[3,256]{1,0:T(4,128)S(1)}, f32[3,256]{1,0:T(4,128)}, u32[]{:S(2)}) copy-start(f32[3,256]{1,0:T(4,128)} %param.20) | copy-start | bytes 9220
  60.5 11.5 %all-to-all-start.3 = ((bf16[32,2,896]{2,1,0:T(2,128)(2,1)}), bf16[32,2,896]{2,1,0:T(2,128)(2,1)S(1)}, u32[]{:S(2)}, u32[]{:S(2)}) async-start(bf16[32,2,896]{2,1,0:T(2,128)(2,1)} %convert_element_type.161), calls=%async_computation.3 | async-start | bytes 229376 | tf_op jit(solution)/shard_map/all_to_all | solution.py:43
  73.0 12.0 %all-to-all-start.4 = ((bf16[32,2,768]{2,1,0:T(2,128)(2,1)}), bf16[32,2,768]{2,1,0:T(2,128)(2,1)S(1)}, u32[]{:S(2)}, u32[]{:S(2)}) async-start(bf16[32,2,768]{2,1,0:T(2,128)(2,1)} %broadcast_in_dim.19), calls=%async_computation.4 | async-start | bytes 196608 | tf_op jit(solution)/shard_map/all_to_all | solution.py:39
  75.6 103.2 %all-gather.7.cloned.1.call-start = ((), (), s32[]{:S(2)}) async-start(), calls=%async_computation.11 | async-start | bytes 2433024 | tf_op jit(solution)/shard_map/all_gather | solution.py:183
  113.5 17.3 %collective-permute-start.4 = (f32[4,256]{1,0:T(4,128)S(1)}, f32[4,256]{1,0:T(4,128)S(1)}, u32[]{:S(2)}, u32[]{:S(2)}) collective-permute-start(f32[4,256]{1,0:T(4,128)S(1)} %pad_maximum_fusion.10), channel_id=1, source_target_pairs={{0,2},{1,3},{2,0},{3,1},{4,6},{5,7},{6,4},{7,5},{8,10},{9,11},{10,... | collective-permute-start | bytes 12296 | tf_op jit(solution)/shard_map/ppermute | solution.py:49
  117.8 8.7 %copy-start.13 = (bf16[256,768]{1,0:T(8,128)(2,1)S(1)}, bf16[256,768]{1,0:T(8,128)(2,1)}, u32[]{:S(2)}) copy-start(bf16[256,768]{1,0:T(8,128)(2,1)} %param.18) | copy-start | bytes 1179652
  120.6 12.9 %all-to-all-start.5 = ((bf16[32,2,896]{2,1,0:T(2,128)(2,1)}), bf16[32,2,896]{2,1,0:T(2,128)(2,1)S(1)}, u32[]{:S(2)}, u32[]{:S(2)}) async-start(bf16[32,2,896]{2,1,0:T(2,128)(2,1)} %convert_element_type.170), calls=%async_computation.5 | async-start | bytes 229376 | tf_op jit(solution)/shard_map/all_to_all | solution.py:43
  123.8 9.6 %collective-permute-start.6 = (bf16[96,384]{1,0:T(8,128)(2,1)S(1)}, bf16[96,384]{1,0:T(8,128)(2,1)S(1)}, u32[]{:S(2)}, u32[]{:S(2)}) collective-permute-start(bf16[96,384]{1,0:T(8,128)(2,1)S(1)} %constant_dynamic-slice_fusion.1), channel_id=1, source_target_pairs={{0,16},{4,20},{8,24},{12,28},{16,0},{20,4},{24,8},{28,12},{1,17},{... | collective-permute-start | bytes 221192 | tf_op jit(solution)/shard_map/ppermute | solution.py:49
  126.5 12.4 %collective-permute-start.2 = (bf16[256,768]{1,0:T(8,128)(2,1)S(1)}, bf16[256,768]{1,0:T(8,128)(2,1)S(1)}, u32[]{:S(2)}, u32[]{:S(2)}) collective-permute-start(bf16[256,768]{1,0:T(8,128)(2,1)S(1)} %copy-done.13), channel_id=1, source_target_pairs={{0,2},{1,3},{2,0},{3,1},{4,6},{5,7},{6,4},{7,5},{8,10},{9,11},{10,... | collective-permute-start | bytes 1179656 | tf_op jit(solution)/shard_map/ppermute | solution.py:49
  134.5 11.8 %all-to-all-start.6 = ((bf16[32,2,768]{2,1,0:T(2,128)(2,1)}), bf16[32,2,768]{2,1,0:T(2,128)(2,1)S(1)}, u32[]{:S(2)}, u32[]{:S(2)}) async-start(bf16[32,2,768]{2,1,0:T(2,128)(2,1)} %broadcast_in_dim.20), calls=%async_computation.6 | async-start | bytes 196608 | tf_op jit(solution)/shard_map/all_to_all | solution.py:39
  146.3 11.8 %collective-permute-start.5 = (f32[2,4,256]{2,1,0:T(4,128)S(1)}, f32[2,4,256]{2,1,0:T(4,128)S(1)}, u32[]{:S(2)}, u32[]{:S(2)}) collective-permute-start(f32[2,4,256]{2,1,0:T(4,128)S(1)} %pad_maximum_fusion.9), channel_id=1, source_target_pairs={{0,1},{1,0},{2,3},{3,2},{4,5},{5,4},{6,7},{7,6},{8,9},{9,8},{10,11... | collective-permute-start | bytes 24584 | tf_op jit(solution)/shard_map/ppermute | solution.py:49
  146.8 11.3 %collective-permute-start.7 = (bf16[2,96,384]{2,1,0:T(8,128)(2,1)S(1)}, bf16[2,96,384]{2,1,0:T(8,128)(2,1)S(1)}, u32[]{:S(2)}, u32[]{:S(2)}) collective-permute-start(bf16[2,96,384]{2,1,0:T(8,128)(2,1)S(1)} %pad_maximum_fusion.6), channel_id=1, source_target_pairs={{0,8},{4,12},{8,0},{12,4},{16,24},{20,28},{24,16},{28,20},{1,9},{5... | collective-permute-start | bytes 442376 | tf_op jit(solution)/shard_map/ppermute | solution.py:49
  150.3 7.8 %copy-start.3 = (f32[64,768]{1,0:T(8,128)}, f32[64,768]{1,0:T(8,128)S(1)}, u32[]{:S(2)}) copy-start(f32[64,768]{1,0:T(8,128)S(1)} %get-tuple-element.22) | copy-start | bytes 589828
  151.8 12.1 %all-to-all-start.7 = ((bf16[32,2,896]{2,1,0:T(2,128)(2,1)}), bf16[32,2,896]{2,1,0:T(2,128)(2,1)S(1)}, u32[]{:S(2)}, u32[]{:S(2)}) async-start(bf16[32,2,896]{2,1,0:T(2,128)(2,1)} %convert_element_type.177), calls=%async_computation.7 | async-start | bytes 229376 | tf_op jit(solution)/shard_map/all_to_all | solution.py:43
  154.3 21.9 %collective-permute-start.3 = (bf16[2,256,768]{2,1,0:T(8,128)(2,1)S(1)}, bf16[2,256,768]{2,1,0:T(8,128)(2,1)S(1)}, u32[]{:S(2)}, u32[]{:S(2)}) collective-permute-start(bf16[2,256,768]{2,1,0:T(8,128)(2,1)S(1)} %pad_maximum_fusion.1), channel_id=1, source_target_pairs={{0,1},{1,0},{2,3},{3,2},{4,5},{5,4},{6,7},{7,6},{8,9},{9,8},{10,11... | collective-permute-start | bytes 2359304 | tf_op jit(solution)/shard_map/ppermute | solution.py:49
  158.2 17.0 %collective-permute-start.8 = (bf16[2,2,96,384]{3,2,1,0:T(8,128)(2,1)S(1)}, bf16[2,2,96,384]{3,2,1,0:T(8,128)(2,1)S(1)}, u32[]{:S(2)}, u32[]{:S(2)}) collective-permute-start(bf16[2,2,96,384]{3,2,1,0:T(8,128)(2,1)S(1)} %pad_maximum_fusion.5), channel_id=1, source_target_pairs={{0,4},{4,0},{8,12},{12,8},{16,20},{20,16},{24,28},{28,24},{1,5},{5... | collective-permute-start | bytes 884744 | tf_op jit(solution)/shard_map/ppermute | solution.py:49
  164.8 10.3 %all-to-all-start.8 = ((bf16[32,2,768]{2,1,0:T(2,128)(2,1)}), bf16[32,2,768]{2,1,0:T(2,128)(2,1)S(1)}, u32[]{:S(2)}, u32[]{:S(2)}) async-start(bf16[32,2,768]{2,1,0:T(2,128)(2,1)} %broadcast_in_dim.21), calls=%async_computation.8 | async-start | bytes 196608 | tf_op jit(solution)/shard_map/all_to_all | solution.py:39
  176.5 1.1 copy-start.2
  176.5 1.1 copy-start.15
  182.6 2.8 %copy-start.4 = (f32[64,768]{1,0:T(8,128)S(1)}, f32[64,768]{1,0:T(8,128)}, u32[]{:S(2)}) copy-start(f32[64,768]{1,0:T(8,128)} %copy-done.3) | copy-start | bytes 589828
  182.6 2.8 %copy-start.6 = (f32[64,2304]{1,0:T(8,128)S(1)}, f32[64,2304]{1,0:T(8,128)}, u32[]{:S(2)}) copy-start(f32[64,2304]{1,0:T(8,128)} %fusion) | copy-start | bytes 1769476
  190.2 1.7 copy-start.11
  191.9 2.2 copy-start.7
  191.9 2.2 copy-start.14
  194.1 6.5 %copy-start.8 = (bf16[1024,768]{1,0:T(8,128)(2,1)S(1)}, bf16[1024,768]{1,0:T(8,128)(2,1)}, u32[]{:S(2)}) copy-start(bf16[1024,768]{1,0:T(8,128)(2,1)} %copy-done.7) | copy-start | bytes 4718596
  204.9 21.2 %all-to-all-start.9 = ((bf16[8,100,384]{2,1,0:T(8,128)(2,1)}), bf16[8,100,384]{2,1,0:T(8,128)(2,1)S(1)}, u32[]{:S(2)}, u32[]{:S(2)}) async-start(bf16[8,100,384]{2,1,0:T(8,128)(2,1)} %pad_maximum_fusion.2), calls=%async_computation.9 | async-start | bytes 1277952 | tf_op jit(solution)/shard_map/all_to_all | solution.py:43
Sparse Core Ops, SparseCore 0:
  11.5 95.3 all-gather.4
  109.7 58.6 all-gather.6
